TPU v7x, 32 devices: a whole 2x2x4 slice. The times are simulated.
32 devices in a mesh: member: 2 (over y), lon: 8 (over z, x), lat: 2 (over core).
Axes of the slice: x: 2, y: 2, z: 4, core: 2. Of those that a mesh axis runs over, the one named last changes fastest.
Arguments:
- state_tokens: bfloat16 [8, 24, 96, 768], P('member', 'lat', 'lon'), parts along dimension 0, may hold values from -32 to 32
- land_mask: int32 [24, 96], P('lat', 'lon'), may hold values 0 or 1
- pad_mask: int32 [24], replicated, may hold values from 0 to 1, as said below
- land_embed: float32 [2, 768], replicated, may hold values from -3 to 3
- w_qkv: bfloat16 [768, 1152], replicated, may hold values from -0.21875 to 0.21875
- w_proj: bfloat16 [384, 768], replicated, may hold values from -0.3125 to 0.3125
- proj_bias: float32 [768], replicated, may hold values from -4 to 4
- norm_gain: float32 [768], replicated, may hold values from 0.5 to 1.5
- norm_shift: float32 [768], replicated, may hold values from -1.5 to 1.5
- bias_table: bfloat16 [4, 2, 12, 3312], P('lat'), may hold values from -3.5 to 320
- index_table: int32 [144, 144], replicated, may hold values from 0 to 3311
Outputs:
- result: bfloat16 [8, 24, 96, 768], P('member', 'lat', 'lon'), parts along dimension 0
There are 2 independent parts, one for each index of `member`. A program takes and returns all parts, laid end to end along the dimension named above; an argument that names none is the same for every part. Nothing has to cross between parts.
Inputs may be any that keep to these rules, and one draw needn't show every extreme that they name: pad_mask is 1 on every row except at most the first 2 and the last 2 of the 24 rows, which are 0 where padded; one of the two ends has exactly 2 padding rows.
All inputs are finite; a program needn't handle non-finite values. No bound on the sum of `land_mask` on one device may be relied on, other than what follows from the above.
Results may differ from a plain program's by a relative error of at most 0.0085.
Values may be sent and summed in bfloat16 or wider, within the bound.
A program may use at most 64 MiB of HBM per device.

v0:
```python
import jax
import jax.numpy as jnp
import numpy as np
from jax import lax
from jax.experimental import pallas as pl
from jax.experimental.pallas import tpu as pltpu
from jax.sharding import PartitionSpec as P

HEADS = 12
HEAD_DIM = 32
WIN_Z = 2
WIN_LAT = 6
WIN_LON = 12
WIN_TOK = 144
HALF_LAT = WIN_LAT // 2
HALF_LON = WIN_LON // 2
GROUP = WIN_Z * HALF_LAT * HALF_LON
SLOT = 48
LOW = 256
SHUT = -1e30
WIDTH = HEADS * HEAD_DIM

norm_epsilon = 1e-05


def from_behind(shard, axis, by):
    size = lax.axis_size(axis)
    return lax.ppermute(shard, axis, [(i, (i + by) % size) for i in range(size)])


def group_tokens(a, b):
    dz, di, dj = np.meshgrid(
        np.arange(WIN_Z), np.arange(HALF_LAT), np.arange(HALF_LON), indexing="ij"
    )
    return ((dz * WIN_LAT + a * HALF_LAT + di) * WIN_LON + b * HALF_LON + dj).reshape(-1)


def window_orders():
    groups = [group_tokens(a, b) for a in range(2) for b in range(2)]
    queries = np.concatenate(groups)
    keys = np.concatenate([g[:32] for g in groups] + [g[32:] for g in groups])
    return queries, keys


def token_orders(levels, lat_rows, lon_columns):
    quarters = lat_rows // HALF_LAT
    z_windows = levels // WIN_Z
    rows = 2 * quarters * z_windows * SLOT
    placed = np.full((rows,), -1, np.int32)
    plain = np.full((rows,), -1, np.int32)
    row = 0
    for lon_half in range(2):
        for quarter in range(quarters):
            for zw in range(z_windows):
                a, b = 1 - quarter % 2, 1 - lon_half
                t = 0
                for dz in range(WIN_Z):
                    for di in range(HALF_LAT):
                        for dj in range(HALF_LON):
                            z = (zw * WIN_Z + dz + WIN_Z // 2) % levels
                            i = quarter * HALF_LAT + di
                            j = lon_half * HALF_LON + dj
                            natural = (z * lat_rows + i) * 16 + j
                            place = t if t < 32 else t + 4 * (2 * a + b)
                            placed[row + place] = natural
                            plain[row + t] = natural
                            t += 1
                row += SLOT
    return placed, plain


def bias_kernel(
    index_ref,
    before_ref,
    own_ref,
    pad_ref,
    lat_ref,
    to_q_ref,
    to_k_ref,
    to_q_rest_ref,
    to_k_rest_ref,
    geometry_ref,
    out_ref,
    low_ref,
    high_ref,
    table_ref,
):
    positions = own_ref.shape[-1]
    highs = table_ref.shape[1] // 48
    half_row = lax.broadcasted_iota(jnp.int32, (8, LOW), 0) < 4
    low_iota = lax.broadcasted_iota(jnp.int32, (LOW, LOW), 0)

    def dot(x, y):
        return jnp.dot(x, y, preferred_element_type=jnp.float32)

    index = index_ref[...]
    rest_lane = lax.broadcasted_iota(jnp.int32, (160, LOW), 1) // 16
    rest_row = lax.broadcasted_iota(jnp.int32, (160, LOW), 0) % 16
    gather = jnp.where(
        lax.broadcasted_iota(jnp.int32, (16, 160), 1) // 16
        == lax.broadcasted_iota(jnp.int32, (16, 160), 0),
        1.0,
        0.0,
    ).astype(jnp.bfloat16)
    for values, ref in ((index % LOW, low_ref), (index // LOW, high_ref)):
        values = values.astype(jnp.float32).astype(jnp.bfloat16)
        main = dot(dot(to_q_ref[...], values).astype(jnp.bfloat16), to_k_ref[...])
        ref[0:WIN_TOK, :] = main.astype(jnp.int32)
        rest = dot(dot(to_q_rest_ref[...], values).astype(jnp.bfloat16), to_k_rest_ref[...])
        rest = jnp.where(rest_lane == rest_row, rest, 0.0).astype(jnp.bfloat16)
        rest = dot(gather, rest).astype(jnp.int32)
        ref[WIN_TOK : WIN_TOK + 16, :] = rest[:, 0:128]
        ref[WIN_TOK + 16 : WIN_TOK + 32, :] = rest[:, 128:256]

    for k in range(highs):
        end = min(positions, (k + 1) * LOW)
        sides = []
        for window in range(3):
            parts = []
            for zw in range(WIN_Z):
                ref = before_ref if window == 0 else own_ref.at[window - 1]
                part = ref[zw, :, k * LOW : end].astype(jnp.float32)
                if end < (k + 1) * LOW:
                    fill = jnp.zeros((part.shape[0], (k + 1) * LOW - end), jnp.float32)
                    part = jnp.concatenate([part, fill], axis=1)
                parts.append(part)
            sides.append([parts[0][:8], parts[1][:8], parts[0][8:], parts[1][8:]])
        for a, edge in ((0, 2), (1, 0)):
            block = jnp.concatenate(sides[edge] + sides[1], axis=0)
            table_ref[a, k * 48 : (k + 1) * 48, :] = block.astype(jnp.bfloat16)

    lat_total = pad_ref.shape[0]
    windows = lat_total // WIN_LAT
    base = 2 * lat_ref[0]

    def look_up(a, tile, low, high):
        hot = jnp.where(low_iota == low, 1.0, 0.0).astype(jnp.bfloat16)
        found = dot(table_ref[a], hot)
        high = jnp.broadcast_to(high, (48, LOW))
        total = found[0:48]
        for k in range(1, highs):
            total = jnp.where(high == k, found[k * 48 : (k + 1) * 48], total)
        geometry = geometry_ref[tile]
        key_row, same_half, same_level = geometry[0:1], geometry[1:2], geometry[2:3]
        pieces = []
        for s in range(2):
            window = base
            if s == 0:
                window = lax.rem(base - 1 + windows if a == 1 else base + 1, windows)
            usable = jnp.zeros((1, LOW), jnp.int32)
            for n in range(WIN_LAT):
                source = lax.rem(window * WIN_LAT + n + HALF_LAT, lat_total)
                usable = jnp.where(key_row == n, pad_ref[source], usable)
            inner = (window != windows - 1).astype(jnp.int32)
            usable = jnp.where(usable == 1, jnp.maximum(same_half, inner), 0)
            first = jnp.broadcast_to(usable, (8, LOW))
            second = jnp.broadcast_to(usable * same_level, (8, LOW))
            for kind, allowed in enumerate((first, second, jnp.where(half_row, first, second))):
                part = total[(s * 3 + kind) * 8 : (s * 3 + kind) * 8 + 8]
                pieces.append(jnp.where(allowed == 1, part, SHUT))
        return pieces

    def both(x, y):
        return jnp.concatenate([x, y], axis=0).astype(jnp.bfloat16)

    for a in range(2):

        def pair(p, carry, a=a):
            tile = a * 36 + p

            def two(ref):
                return jnp.concatenate(
                    [ref[pl.ds(2 * tile, 1), :], ref[pl.ds(2 * tile + 1, 1), :]], axis=1
                )

            pieces = look_up(a, tile, two(low_ref), two(high_ref))
            for s in range(2):
                for kind in range(3):
                    part = pieces[s * 3 + kind]
                    out_ref[a, s, kind, p, :, 0:128] = both(part[:, 0:128], part[:, 128:256])
            return carry

        lax.fori_loop(0, 36, pair, 0)
        for tile in range(5):
            row = WIN_TOK + a * 5 + tile

            def wide(ref, row=row):
                return jnp.concatenate([ref[row : row + 1, :], ref[row + 16 : row + 17, :]], axis=1)

            pieces = look_up(a, 72 + a * 5 + tile, wide(low_ref), wide(high_ref))
            for j in range(0, 16, 2):
                q = tile * 16 + j
                if q < 72:
                    for s in range(2):
                        for kind in range(3):
                            part = pieces[s * 3 + kind]
                            out_ref[a, s, kind, q // 2, :, 128:144] = both(
                                part[:, 16 * j : 16 * j + 16], part[:, 16 * j + 16 : 16 * j + 32]
                            )


def attend_kernel(
    bias_ref,
    own_ref,
    left_ref,
    right_ref,
    up_ref,
    down_ref,
    hidden_ref,
    restore_ref,
    w_ref,
    offset_ref,
    gain_ref,
    shift_ref,
    out_ref,
    keys_ref,
    attended_ref,
):
    step = pl.program_id(0)

    @pl.when(step == 0)
    def _():
        def column(c, quarter, zw):
            if quarter < 0:
                return up_ref.at[c, zw]
            if quarter > 3:
                return down_ref.at[c, zw]
            if c == 0:
                return left_ref.at[quarter, zw]
            if c == 3:
                return right_ref.at[quarter, zw]
            return own_ref.at[c - 1, quarter, zw, :, WIDTH : 3 * WIDTH]

        for lat in range(3):
            for lon in range(2):
                for zw in range(2):
                    rest = None
                    for a in range(2):
                        for b in range(2):
                            ref = column(2 * lon + b, 2 * lat - 1 + a, zw)
                            n = 32 * (2 * a + b)
                            keys_ref[2 * lat + lon, zw, n : n + 32, :] = ref[0:32, :]
                            tail = ref[32:48, :]
                            rest = tail if rest is None else rest + tail
                    keys_ref[2 * lat + lon, zw, 128:144, :] = rest

    quarter, lon = step // 2, step % 2
    window = 2 * ((quarter + 1) // 2) + lon
    head_mask = jnp.where(
        lax.broadcasted_iota(jnp.int32, (8, 256), 1) // HEAD_DIM
        == lax.broadcasted_iota(jnp.int32, (8, 256), 0),
        1.0,
        0.0,
    )
    gather_rows = jnp.where(
        lax.broadcasted_iota(jnp.int32, (SLOT, 8 * GROUP), 1) // 8
        == lax.broadcasted_iota(jnp.int32, (SLOT, 8 * GROUP), 0),
        1.0,
        0.0,
    ).astype(jnp.bfloat16)
    queries = []
    for zw in range(2):
        q = own_ref[lon, quarter, zw, :, 0:WIDTH].astype(jnp.float32)
        tail = (q[32:36] + q[36:40]) + (q[40:44] + q[44:48])
        queries.append(jnp.concatenate([q[0:32], tail], axis=0))
    results = []
    for kind in range(3):
        if kind < 2:
            q = queries[kind][:, 0:256]
            key = keys_ref[window, kind, :, 0:256]
            value = keys_ref[window, kind, :, WIDTH : WIDTH + 256]
        else:
            q = jnp.concatenate([queries[0][:, 256:384], queries[1][:, 256:384]], axis=1)
            key = jnp.concatenate(
                [keys_ref[window, 0, :, 256:384], keys_ref[window, 1, :, 256:384]], axis=1
            )
            value = jnp.concatenate(
                [keys_ref[window, 0, :, 640:768], keys_ref[window, 1, :, 640:768]], axis=1
            )
        spread = (q[:, None, :] * head_mask[None]).reshape(8 * GROUP, 256).astype(jnp.bfloat16)
        scores = lax.dot_general(
            spread, key, (((1,), (1,)), ((), ())), preferred_element_type=jnp.float32
        )
        bias = bias_ref[0, 0, kind].reshape(8 * GROUP, 256)[:, 0:WIN_TOK]
        bias = bias.astype(jnp.float32)
        scores = scores * (HEAD_DIM**-0.5) + bias
        powers = jnp.exp(scores - jnp.max(scores, axis=-1, keepdims=True))
        weights = (powers / jnp.sum(powers, axis=-1, keepdims=True)).astype(jnp.bfloat16)
        mixed = jnp.dot(weights, value, preferred_element_type=jnp.float32)
        mixed = (mixed.reshape(GROUP, 8, 256) * head_mask[None]).reshape(8 * GROUP, 256)
        results.append(
            jnp.dot(
                gather_rows, mixed.astype(jnp.bfloat16), preferred_element_type=jnp.float32
            ).astype(jnp.bfloat16)
        )
    for zw in range(2):
        row = ((lon * 4 + quarter) * 2 + zw) * SLOT
        row = pl.multiple_of(row, SLOT)
        attended_ref[pl.ds(row, SLOT), 0:256] = results[zw]
        attended_ref[pl.ds(row, SLOT), 256:384] = results[2][:, zw * 128 : zw * 128 + 128]

    @pl.when(step == pl.num_programs(0) - 1)
    def _():
        chunk = 192
        for n in range(0, hidden_ref.shape[0], chunk):
            natural = jnp.dot(
                restore_ref[n : n + chunk, :],
                attended_ref[...],
                preferred_element_type=jnp.float32,
            ).astype(jnp.bfloat16)
            projected = (
                jnp.dot(natural, w_ref[...], preferred_element_type=jnp.float32)
                + offset_ref[...]
            )
            centered = projected - jnp.mean(projected, axis=-1, keepdims=True)
            spread = jnp.mean(centered * centered, axis=-1, keepdims=True)
            normed = (
                centered * lax.rsqrt(spread + norm_epsilon) * gain_ref[...]
                + shift_ref[...]
            )
            result = (hidden_ref[n : n + chunk, :].astype(jnp.float32) + normed).astype(
                jnp.bfloat16
            )
            result = result.reshape(chunk // 16, 16, result.shape[-1])
            out_ref[n // 16 : (n + chunk) // 16] = result[:, : out_ref.shape[1], :]


def as_tiles(rows):
    main = rows[:, :128].reshape(72, 256)
    rest = np.pad(rows[:, 128:].reshape(2, 72, 16), ((0, 0), (0, 8), (0, 0))).reshape(10, 256)
    return np.concatenate([main, rest], axis=0)


def bias_constants():
    queries, keys = window_orders()
    eye = np.eye(WIN_TOK, dtype=np.float32)
    to_q = eye[queries]
    to_q_rest = np.pad(to_q.reshape(2, 72, WIN_TOK), ((0, 0), (0, 8), (0, 0)))
    to_q_rest = to_q_rest.reshape(160, WIN_TOK)
    to_k = eye[keys[:128]].T
    to_k_rest = eye[np.tile(keys[128:], 16)].T
    q_level, q_half = queries // 72, queries // 12 % 6 // 3
    k_level, k_row = keys // 72, keys // 12 % 6
    planes = [
        np.broadcast_to(k_row[None, :], (WIN_TOK, WIN_TOK)),
        q_half[:, None] == (k_row // 3)[None, :],
        q_level[:, None] == k_level[None, :],
    ]
    geometry = np.stack([as_tiles(p.astype(np.int32)) for p in planes], axis=1)
    matrices = [jnp.asarray(m, jnp.bfloat16) for m in (to_q, to_k, to_q_rest, to_k_rest)]
    return matrices + [jnp.asarray(geometry)]


def on_device(
    state_tokens,
    land_mask,
    pad_mask,
    land_embed,
    w_qkv,
    w_proj,
    proj_bias,
    norm_gain,
    norm_shift,
    bias_table,
    index_table,
):
    levels, lat_rows, lon_columns, features = state_tokens.shape
    assert (levels, lat_rows, lon_columns) == (2 * WIN_Z, 2 * WIN_LAT, WIN_LON)
    lat_total = lat_rows * lax.axis_size("lat")
    embedded = jnp.where(land_mask[:, :, None] == 1, land_embed[1], land_embed[0])
    hidden = (state_tokens.astype(jnp.float32) + embedded[None]).astype(jnp.bfloat16)
    hidden = jnp.pad(hidden, ((0, 0), (0, 0), (0, 16 - lon_columns), (0, 0)))
    hidden = hidden.reshape(levels * lat_rows * 16, features)
    rows = hidden.shape[0]
    placed, plain = token_orders(levels, lat_rows, lon_columns)
    natural = jnp.arange(rows, dtype=jnp.int32)
    to_groups = (jnp.asarray(placed)[:, None] == natural[None, :]).astype(jnp.bfloat16)
    restore = (natural[:, None] == jnp.asarray(plain)[None, :]).astype(jnp.bfloat16)
    grouped = jnp.dot(to_groups, hidden, preferred_element_type=jnp.float32).astype(jnp.bfloat16)
    shape = (2, 4, 2, SLOT)
    qkv = jnp.dot(grouped, w_qkv, preferred_element_type=jnp.float32)
    qkv = qkv.astype(jnp.bfloat16).reshape(2, 4, 2, SLOT, 3 * WIDTH)
    kv = qkv[..., WIDTH:]
    right = from_behind(kv[0], "lon", -1)
    left = from_behind(kv[1], "lon", 1)
    up = from_behind(jnp.stack([left[3], kv[0, 3], kv[1, 3], right[3]]), "lat", 1)
    down = from_behind(jnp.stack([left[0], kv[0, 0], kv[1, 0], right[0]]), "lat", -1)
    before = from_behind(bias_table[-1], "lat", 1)
    lat_index = lax.axis_index("lat").astype(jnp.int32).reshape(1)
    in_vmem = pl.BlockSpec(memory_space=pltpu.VMEM)
    in_smem = pl.BlockSpec(memory_space=pltpu.SMEM)
    highs = -(-bias_table.shape[-1] // LOW)
    bias = pl.pallas_call(
        bias_kernel,
        out_shape=jax.ShapeDtypeStruct((2, 2, 3, 36, 16, 256), jnp.bfloat16),
        in_specs=[in_vmem] * 3 + [in_smem] * 2 + [in_vmem] * 5,
        out_specs=in_vmem,
        scratch_shapes=[
            pltpu.VMEM((WIN_TOK + 32, 128), jnp.int32),
            pltpu.VMEM((WIN_TOK + 32, 128), jnp.int32),
            pltpu.VMEM((2, highs * 48, LOW), jnp.bfloat16),
        ],
        compiler_params=pltpu.CompilerParams(vmem_limit_bytes=24 << 20),
        cost_estimate=pl.CostEstimate(
            flops=2 * 82 * 624 * 256 * 256, bytes_accessed=8 << 20, transcendentals=0
        ),
        name="bias",
    )(index_table, before, bias_table, pad_mask, lat_index, *bias_constants())
    vectors = [v.reshape(1, features) for v in (proj_bias, norm_gain, norm_shift)]
    whole = pl.BlockSpec(memory_space=pltpu.VMEM)

    def bias_block(i):
        quarter, lon = i // 2, i % 2
        return (1 - quarter % 2, (quarter + 1) // 2 % 2, 0, 1 - lon, 0, 0)

    out = pl.pallas_call(
        attend_kernel,
        grid=(8,),
        out_shape=jax.ShapeDtypeStruct((levels * lat_rows, lon_columns, features), jnp.bfloat16),
        in_specs=[pl.BlockSpec((1, 1, 3, GROUP // 2, 16, 256), bias_block)] + [whole] * 11,
        out_specs=whole,
        scratch_shapes=[
            pltpu.VMEM((6, 2, WIN_TOK, 2 * WIDTH), jnp.bfloat16),
            pltpu.VMEM((rows, WIDTH), jnp.bfloat16),
        ],
        compiler_params=pltpu.CompilerParams(
            vmem_limit_bytes=40 << 20, dimension_semantics=("arbitrary",)
        ),
        name="attend",
    )(bias, qkv, left, right, up, down, hidden, restore, w_proj, *vectors)
    return out.reshape(state_tokens.shape)


def solution(mesh):
    in_specs = (
        P("member", "lat", "lon", None),
        P("lat", "lon"),
        P(),
        P(),
        P(),
        P(),
        P(),
        P(),
        P(),
        P("lat", None, None, None),
        P(),
    )
    out_specs = P("member", "lat", "lon", None)
    return jax.shard_map(
        on_device, mesh=mesh, in_specs=in_specs, out_specs=out_specs, check_vma=False
    )
```

profile of v0, /device:TPU:0, one launch (start us, length us, event | category | flops | bytes accessed | tf_op | source)
XLA Modules:
  0.0 80.9 jit_solution(6533350264573457748)
XLA Ops:
  0.0 0.0 copy-start
  0.0 0.8 %broadcast_compare_fusion = pred[12,12]{1,0:T(8,128)(4,1)S(1)} fusion(s32[12,12]{1,0:T(8,128)} %param.19), kind=kLoop, calls=%fused_computation.18 | loop fusion | flops 144 | bytes 720 | tf_op jit(solution)/shard_map/eq | solution.py:370
  0.8 0.8 slice_reduce_fusion.1
  1.6 0.1 broadcast_select_fusion
  1.7 1.6 %add_convert_fusion = bf16[4,12,12,768]{3,0,2,1:T(4,128)(2,1)S(1)} fusion(bf16[4,12,12,768]{3,0,2,1:T(4,128)(2,1)} %param.18, f32[12,12,768]{2,1,0:T(8,128)S(1)} %broadcast_select_fusion), kind=kLoop, calls=%fused_computation.5 | loop fusion | flops 1327104 | bytes 2211840 | tf_op jit(solution)/shard_map/convert_element_type | solution.py:371
  3.4 0.0 copy-start.21
  3.4 0.1 copy.23
  3.5 1.2 %pad.4.clone = bf16[4,12,16,768]{3,2,1,0:T(8,128)(2,1)} pad(bf16[4,12,12,768]{3,2,1,0:T(8,128)(2,1)S(1)} %copy.23, bf16[]{:T(256)} %constant.22.clone.1), padding=0_0x0_0x0_4x0_0 | pad | bytes 2064386 | tf_op jit(solution)/shard_map/jit(_pad)/pad | solution.py:372
  4.7 0.0 copy-done
  4.7 0.0 copy-done.21
  4.7 4.0 %convolution_convert_fusion = bf16[768,1152]{1,0:T(8,128)(2,1)S(1)} fusion(bf16[768,1152]{1,0:T(8,128)(2,1)S(1)} %copy-done, bf16[768,768]{1,0:T(8,128)(2,1)} %bitcast.23, s32[768]{0:T(1024)S(1)} %copy-done.21), kind=kOutput, calls=%fused_computation | convolution fusion | flops 2266988544 | bytes 4721664 | tf_op jit(solution)/shard_map/dot_general | solution.py:381
  8.7 0.0 copy-start.16
  8.8 1.1 %slice_bitcast_fusion = (bf16[4,2,48,768]{3,2,1,0:T(8,128)(2,1)}, bf16[4,2,48,768]{3,2,1,0:T(8,128)(2,1)}) fusion(bf16[2,4,2,48,1152]{4,3,2,1,0:T(8,128)(2,1)S(1)} %bitcast.20), kind=kLoop, calls=%fused_computation.8 | loop fusion | bytes 2359296 | tf_op jit(solution)/shard_map/squeeze | solution.py:384
  9.9 6.1 %collective-permute-start.2 = (bf16[4,2,48,768]{3,2,1,0:T(8,128)(2,1)}, bf16[4,2,48,768]{3,2,1,0:T(8,128)(2,1)}, u32[]{:S(2)}, u32[]{:S(2)}) collective-permute-start(bf16[4,2,48,768]{3,2,1,0:T(8,128)(2,1)} %get-tuple-element.11), channel_id=1, source_target_pairs={{0,14},{2,0},{4,2},{6,4},{8,6},{10,8},{12,10},{14,12},{1,15},{3,1}... | collective-permute-start | bytes 1769480 | tf_op jit(solution)/shard_map/ppermute | solution.py:28
  15.9 0.0 copy-done.16
  16.0 0.7 slice_bitcast_fusion.2
  16.7 0.8 copy-done.2
  17.4 0.0 collective-permute-start
  17.4 0.0 collective-permute-start.1
  17.5 0.8 %slice_bitcast_fusion.4 = (bf16[1,2,48,768]{3,2,1,0:T(8,128)(2,1)}, bf16[1,2,48,768]{3,2,1,0:T(8,128)(2,1)}, bf16[1,2,48,768]{3,2,1,0:T(8,128)(2,1)}, bf16[1,2,48,768]{3,2,1,0:T(8,128)(2,1)}) fusion(bf16[2,4,2,48,1152]{4,3,2,1,0:T(8,128)(2,1)S(1)} %bitcast.21), kind=kLoop, calls=%fused_computation.15 | loop fusion | bytes 1179648 | tf_op jit(solution)/shard_map/stack;squeeze | solution.py:387
  18.3 0.0 copy-done.18
  18.3 0.0 copy-done.19
  18.3 0.0 copy-done.20
  18.3 0.0 copy-done.17
  18.4 0.0 copy-start.12
  18.4 0.0 copy-start.13
  18.4 0.4 fusion.1.restore_ref
  18.8 0.0 copy-start.3
  18.8 0.0 copy-start.5
  18.8 0.0 copy-start.6
  18.8 0.0 copy-start.7
  18.8 0.0 copy-start.8
  18.9 0.0 copy-start.9
  18.9 0.0 copy-start.10
  18.9 0.0 copy-start.11
  18.9 20.3 %collective-permute-done.2.right_ref = bf16[4,2,48,768]{3,2,1,0:T(8,128)(2,1)} collective-permute-done((bf16[4,2,48,768]{3,2,1,0:T(8,128)(2,1)}, bf16[4,2,48,768]{3,2,1,0:T(8,128)(2,1)}, u32[]{:S(2)}, u32[]{:S(2)}) %collective-permute-start.2) | collective-permute-done | bytes 589856 | tf_op jit(solution)/shard_map/ppermute | solution.py:28
  39.2 1.0 %fusion.5 = (bf16[1,2,48,768]{3,2,1,0:T(8,128)(2,1)S(1)}, bf16[1,2,48,768]{3,2,1,0:T(8,128)(2,1)S(1)}) fusion(bf16[4,2,48,768]{3,2,1,0:T(8,128)(2,1)} %collective-permute-done.2.right_ref), kind=kLoop, calls=%fused_computation.22 | loop fusion | bytes 589824 | tf_op jit(solution)/shard_map/slice | solution.py:387
  40.2 0.0 collective-permute-done.1.left_ref
  40.2 1.0 %fusion.4 = (bf16[1,2,48,768]{3,2,1,0:T(8,128)(2,1)S(1)}, bf16[1,2,48,768]{3,2,1,0:T(8,128)(2,1)S(1)}) fusion(bf16[4,2,48,768]{3,2,1,0:T(8,128)(2,1)} %collective-permute-done.1.left_ref), kind=kLoop, calls=%fused_computation.21 | loop fusion | bytes 589824 | tf_op jit(solution)/shard_map/slice | solution.py:387
  41.2 0.0 copy-done.14
  41.2 0.0 copy-done.15
  41.2 0.1 pad_maximum_fusion
  41.3 0.1 collective-permute-start.3
  41.4 0.0 copy-done.12
  41.4 0.0 copy-done.13
  41.4 0.1 pad_maximum_fusion.1
  41.5 0.5 collective-permute-start.4
  42.0 0.0 collective-permute-done.before_ref
  42.0 0.0 copy-done.5
  42.0 0.0 copy-done.6
  42.1 0.0 copy-done.7
  42.1 0.0 copy-done.8
  42.1 0.0 copy-done.9
  42.1 0.0 copy-done.10
  42.1 0.0 copy-done.11
  42.1 0.0 copy-start.1
  42.1 0.0 copy-start.4
  42.1 22.1 %bias.1.bias_ref = bf16[2,2,3,36,16,256]{5,4,3,2,1,0:T(8,128)(2,1)S(1)} custom-call(s32[144,144]{1,0:T(8,128)S(1)} %copy-done.5, bf16[2,12,3312]{2,1,0:T(8,128)(2,1)} %collective-permute-done.before_ref, bf16[2,2,12,3312]{3,2,1,0:T(8,128)(2,1)S(1)} %copy-done.3, s32[24]{0:T(128)S(1)} %copy-done.6, s32[1]{0:T(128)} %bitcast.1.lat_ref, ...), custom_call_target="tpu_custom_call" | custom-call | flops 6706692096 | bytes 8388608 | tf_op jit(solution)/shard_map/bias/pallas_call | solution.py:393
  64.3 0.0 collective-permute-done.3.up_ref
  64.3 0.0 collective-permute-done.4.down_ref
  64.3 0.0 copy-done.1
  64.3 0.0 copy-done.4
  64.3 15.0 %attend.1 = bf16[48,12,768]{2,1,0:T(8,128)(2,1)S(1)} custom-call(bf16[2,2,3,36,16,256]{5,4,3,2,1,0:T(8,128)(2,1)S(1)} %bias.1.bias_ref, bf16[2,4,2,48,1152]{4,3,2,1,0:T(8,128)(2,1)S(1)} %bitcast.22, bf16[4,2,48,768]{3,2,1,0:T(8,128)(2,1)} %collective-permute-done.1.left_ref, bf16[4,2,48,768]{3,2,1,0:T(8,128)(2,1)} %collective-permute-done.2.right_ref, ...), custom_call_target="tpu_custom_call" | custom-call | tf_op jit(solution)/shard_map/attend/pallas_call | solution.py:416
  79.3 1.6 %copy.22 = bf16[4,12,12,768]{3,0,2,1:T(4,128)(2,1)} copy(bf16[4,12,12,768]{3,2,1,0:T(8,128)(2,1)S(1)} %bitcast.25) | data formatting | bytes 1769472 | tf_op jit(solution)/shard_map/reshape | solution.py:431
  (12 shorter events, 0.1 us)
Async XLA Ops:
  0.0 4.7 %copy-start = (bf16[768,1152]{1,0:T(8,128)(2,1)S(1)}, bf16[768,1152]{1,0:T(8,128)(2,1)}, u32[]{:S(2)}) copy-start(bf16[768,1152]{1,0:T(8,128)(2,1)} %param.22) | copy-start | bytes 5308420
  3.4 1.3 %copy-start.21 = (s32[768]{0:T(1024)S(1)}, s32[768]{0:T(1024)}, u32[]{:S(2)}) copy-start(s32[768]{0:T(1024)} %constant.23.clone) | copy-start | bytes 9220
  8.7 7.2 %copy-start.16 = (bf16[2,2,12,3312]{3,1,2,0:T(2,128)(2,1)S(1)}, bf16[2,2,12,3312]{3,1,2,0:T(2,128)(2,1)}, u32[]{:S(2)}) copy-start(bf16[2,2,12,3312]{3,1,2,0:T(2,128)(2,1)} %param.27) | copy-start | bytes 953860
  9.9 8.4 %copy-start.18 = (f32[768]{0:T(1024)S(1)}, f32[768]{0:T(1024)}, u32[]{:S(2)}) copy-start(f32[768]{0:T(1024)} %param.24) | copy-start | bytes 9220
  9.9 8.4 %copy-start.19 = (f32[768]{0:T(1024)S(1)}, f32[768]{0:T(1024)}, u32[]{:S(2)}) copy-start(f32[768]{0:T(1024)} %param.25) | copy-start | bytes 9220
  9.9 8.5 %copy-start.20 = (f32[768]{0:T(1024)S(1)}, f32[768]{0:T(1024)}, u32[]{:S(2)}) copy-start(f32[768]{0:T(1024)} %param.26) | copy-start | bytes 9220
  9.9 8.5 %copy-start.17 = (s32[768]{0:T(1024)S(1)}, s32[768]{0:T(1024)}, u32[]{:S(2)}) copy-start(s32[768]{0:T(1024)} %constant.24.clone) | copy-start | bytes 9220
  9.9 29.3 %collective-permute-start.2 = (bf16[4,2,48,768]{3,2,1,0:T(8,128)(2,1)}, bf16[4,2,48,768]{3,2,1,0:T(8,128)(2,1)}, u32[]{:S(2)}, u32[]{:S(2)}) collective-permute-start(bf16[4,2,48,768]{3,2,1,0:T(8,128)(2,1)} %get-tuple-element.11), channel_id=1, source_target_pairs={{0,14},{2,0},{4,2},{6,4},{8,6},{10,8},{12,10},{14,12},{1,15},{3,1}... | collective-permute-start | bytes 1769480 | tf_op jit(solution)/shard_map/ppermute | solution.py:28
  16.7 0.8 copy-start.2
  17.4 24.6 %collective-permute-start = (bf16[2,12,3312]{2,1,0:T(8,128)(2,1)}, bf16[2,12,3312]{2,1,0:T(8,128)(2,1)}, u32[]{:S(2)}, u32[]{:S(2)}) collective-permute-start(bf16[2,12,3312]{2,1,0:T(8,128)(2,1)} %slice_bitcast_fusion.2), channel_id=1, source_target_pairs={{0,1},{1,0},{2,3},{3,2},{4,5},{5,4},{6,7},{7,6},{8,9},{9,8},{10,11... | collective-permute-start | bytes 476936 | tf_op jit(solution)/shard_map/ppermute | solution.py:28
  17.4 22.7 %collective-permute-start.1 = (bf16[4,2,48,768]{3,2,1,0:T(8,128)(2,1)}, bf16[4,2,48,768]{3,2,1,0:T(8,128)(2,1)}, u32[]{:S(2)}, u32[]{:S(2)}) collective-permute-start(bf16[4,2,48,768]{3,2,1,0:T(8,128)(2,1)} %get-tuple-element.12), channel_id=1, source_target_pairs={{0,2},{2,4},{4,6},{6,8},{8,10},{10,12},{12,14},{14,0},{1,3},{3,5},... | collective-permute-start | bytes 1769480 | tf_op jit(solution)/shard_map/ppermute | solution.py:28
  18.3 22.9 %copy-start.14 = (bf16[1,2,48,768]{3,2,1,0:T(8,128)(2,1)S(1)}, bf16[1,2,48,768]{3,2,1,0:T(8,128)(2,1)}, u32[]{:S(2)}) copy-start(bf16[1,2,48,768]{3,2,1,0:T(8,128)(2,1)} %get-tuple-element.9) | copy-start | bytes 442372
  18.3 22.9 %copy-start.15 = (bf16[1,2,48,768]{3,2,1,0:T(8,128)(2,1)S(1)}, bf16[1,2,48,768]{3,2,1,0:T(8,128)(2,1)}, u32[]{:S(2)}) copy-start(bf16[1,2,48,768]{3,2,1,0:T(8,128)(2,1)} %get-tuple-element.10) | copy-start | bytes 442372
  18.4 23.0 %copy-start.12 = (bf16[1,2,48,768]{3,2,1,0:T(8,128)(2,1)S(1)}, bf16[1,2,48,768]{3,2,1,0:T(8,128)(2,1)}, u32[]{:S(2)}) copy-start(bf16[1,2,48,768]{3,2,1,0:T(8,128)(2,1)} %get-tuple-element.7) | copy-start | bytes 442372
  18.4 23.0 %copy-start.13 = (bf16[1,2,48,768]{3,2,1,0:T(8,128)(2,1)S(1)}, bf16[1,2,48,768]{3,2,1,0:T(8,128)(2,1)}, u32[]{:S(2)}) copy-start(bf16[1,2,48,768]{3,2,1,0:T(8,128)(2,1)} %get-tuple-element.8) | copy-start | bytes 442372
  18.8 23.2 %copy-start.3 = (bf16[2,2,12,3312]{3,2,1,0:T(8,128)(2,1)S(1)}, bf16[2,2,12,3312]{3,2,1,0:T(8,128)(2,1)}, u32[]{:S(2)}) copy-start(bf16[2,2,12,3312]{3,2,1,0:T(8,128)(2,1)} %copy-done.2) | copy-start | bytes 953860
  18.8 23.2 %copy-start.5 = (s32[144,144]{1,0:T(8,128)S(1)}, s32[144,144]{1,0:T(8,128)}, u32[]{:S(2)}) copy-start(s32[144,144]{1,0:T(8,128)} %index_ref.1) | copy-start | bytes 248836
  18.8 23.2 %copy-start.6 = (s32[24]{0:T(128)S(1)}, s32[24]{0:T(128)}, u32[]{:S(2)}) copy-start(s32[24]{0:T(128)} %pad_ref.1) | copy-start | bytes 292
  18.8 23.2 %copy-start.7 = (s32[82,3,256]{2,1,0:T(4,128)S(1)}, s32[82,3,256]{2,1,0:T(4,128)}, u32[]{:S(2)}) copy-start(s32[82,3,256]{2,1,0:T(4,128)} %constant.29.clone.geometry_ref) | copy-start | bytes 755716
  18.8 23.2 %copy-start.8 = (bf16[160,144]{1,0:T(8,128)(2,1)S(1)}, bf16[160,144]{1,0:T(8,128)(2,1)}, u32[]{:S(2)}) copy-start(bf16[160,144]{1,0:T(8,128)(2,1)} %constant.27.clone.to_q_rest_ref) | copy-start | bytes 138244
  18.9 23.2 %copy-start.9 = (bf16[144,256]{1,0:T(8,128)(2,1)S(1)}, bf16[144,256]{1,0:T(8,128)(2,1)}, u32[]{:S(2)}) copy-start(bf16[144,256]{1,0:T(8,128)(2,1)} %constant.28.clone.to_k_rest_ref) | copy-start | bytes 221188
  18.9 23.2 %copy-start.10 = (bf16[144,144]{1,0:T(8,128)(2,1)S(1)}, bf16[144,144]{1,0:T(8,128)(2,1)}, u32[]{:S(2)}) copy-start(bf16[144,144]{1,0:T(8,128)(2,1)} %constant.25.clone.to_q_ref) | copy-start | bytes 124420
  18.9 23.2 %copy-start.11 = (bf16[144,128]{1,0:T(8,128)(2,1)S(1)}, bf16[144,128]{1,0:T(8,128)(2,1)}, u32[]{:S(2)}) copy-start(bf16[144,128]{1,0:T(8,128)(2,1)} %constant.26.clone.to_k_ref) | copy-start | bytes 110596
  41.3 22.9 %collective-permute-start.3 = (bf16[4,2,48,768]{3,2,1,0:T(8,128)(2,1)S(1)}, bf16[4,2,48,768]{3,2,1,0:T(8,128)(2,1)S(1)}, u32[]{:S(2)}, u32[]{:S(2)}) collective-permute-start(bf16[4,2,48,768]{3,2,1,0:T(8,128)(2,1)S(1)} %pad_maximum_fusion), channel_id=1, source_target_pairs={{0,1},{1,0},{2,3},{3,2},{4,5},{5,4},{6,7},{7,6},{8,9},{9,8},{10,11... | collective-permute-start | bytes 1769480 | tf_op jit(solution)/shard_map/ppermute | solution.py:28
  41.5 22.8 %collective-permute-start.4 = (bf16[4,2,48,768]{3,2,1,0:T(8,128)(2,1)S(1)}, bf16[4,2,48,768]{3,2,1,0:T(8,128)(2,1)S(1)}, u32[]{:S(2)}, u32[]{:S(2)}) collective-permute-start(bf16[4,2,48,768]{3,2,1,0:T(8,128)(2,1)S(1)} %pad_maximum_fusion.1), channel_id=1, source_target_pairs={{0,1},{1,0},{2,3},{3,2},{4,5},{5,4},{6,7},{7,6},{8,9},{9,8},{10,11... | collective-permute-start | bytes 1769480 | tf_op jit(solution)/shard_map/ppermute | solution.py:28
  42.1 22.2 %copy-start.1 = (bf16[4,12,16,768]{3,2,1,0:T(8,128)(2,1)S(1)}, bf16[4,12,16,768]{3,2,1,0:T(8,128)(2,1)}, u32[]{:S(2)}) copy-start(bf16[4,12,16,768]{3,2,1,0:T(8,128)(2,1)} %pad.4.clone) | copy-start | bytes 3538948
  42.1 22.2 %copy-start.4 = (bf16[384,768]{1,0:T(8,128)(2,1)S(1)}, bf16[384,768]{1,0:T(8,128)(2,1)}, u32[]{:S(2)}) copy-start(bf16[384,768]{1,0:T(8,128)(2,1)} %w_ref.1) | copy-start | bytes 1769476
where the time goes:
time: 81.9 us; the launch traced here: 80.9 us
  Pallas kernels  37.1 us (45%)
  waiting for transfers between devices  20.3 us (25%)
  local copies, waits for them, and re-layouts  9.26 us (11%)
  starting transfers between devices  6.68 us (8%)
  matrix products  4.04 us (5%)
  other arithmetic  3.13 us (4%)
    pallas_call x1, Pallas kernels, on_device(): pl.pallas_call(bias_kernel, out_shape=jax.ShapeDtypeStruct((2, 2, 3, 36,...  22.1 us
    ppermute x5, waiting for transfers between devices, from_behind(): lax.ppermute(shard, axis, [(i, (i + by) % size) for i in range(size)])  20.3 us
    pallas_call x1, Pallas kernels, on_device(): pl.pallas_call(attend_kernel, grid=(8,), out_shape=jax.ShapeDtypeStruct((...  15 us
    ppermute x5, starting transfers between devices, from_behind(): lax.ppermute(shard, axis, [(i, (i + by) % size) for i in range(size)])  6.68 us
    dot_general x1, matrix products, on_device(): qkv = jnp.dot(grouped, w_qkv, preferred_element_type=jnp.float32)  4.04 us
  transfers between devices with their start and end apart: 5, of which 1 were waited for; matrix products, arithmetic and copies ran while one was open for 5% of the time, Pallas kernels for 27%

commit v1 on v0

v1 whole, which is shorter than its diff:
```python
import functools

import jax
import jax.numpy as jnp
import numpy as np
from jax import lax
from jax.experimental import pallas as pl
from jax.experimental.pallas import tpu as pltpu
from jax.sharding import PartitionSpec as P

HEADS = 12
HEAD_DIM = 32
WIN_Z = 2
WIN_LAT = 6
WIN_LON = 12
WIN_TOK = 144
HALF_LAT = WIN_LAT // 2
HALF_LON = WIN_LON // 2
GROUP = WIN_Z * HALF_LAT * HALF_LON
PAIR = WIN_Z * GROUP
SLOT = 48
EDGE_ROWS = 80
LOW = 256
SHUT = -1e30
WIDTH = HEADS * HEAD_DIM
MESH = pl.DeviceIdType.MESH

norm_epsilon = 1e-05


def group_tokens(a, b):
    dz, di, dj = np.meshgrid(
        np.arange(WIN_Z), np.arange(HALF_LAT), np.arange(HALF_LON), indexing="ij"
    )
    return ((dz * WIN_LAT + a * HALF_LAT + di) * WIN_LON + b * HALF_LON + dj).reshape(-1)


def window_orders():
    groups = [group_tokens(a, b) for a in range(2) for b in range(2)]
    queries = np.concatenate(groups)
    keys = np.concatenate([g[:32] for g in groups] + [g[32:] for g in groups])
    return queries, keys


def dot(x, y):
    return jnp.dot(x, y, preferred_element_type=jnp.float32)


def iota(shape, axis):
    return lax.broadcasted_iota(jnp.int32, shape, axis)


def index_planes(index_ref, to_q_ref, to_k_ref, to_q_rest_ref, to_k_rest_ref, low_ref, high_ref):
    index = index_ref[...]
    rest_lane = iota((160, LOW), 1) // 16
    rest_row = iota((160, LOW), 0) % 16
    gather = jnp.where(iota((16, 160), 1) // 16 == iota((16, 160), 0), 1.0, 0.0)
    gather = gather.astype(jnp.bfloat16)
    for values, ref in ((index % LOW, low_ref), (index // LOW, high_ref)):
        values = values.astype(jnp.float32).astype(jnp.bfloat16)
        main = dot(dot(to_q_ref[...], values).astype(jnp.bfloat16), to_k_ref[...])
        ref[0:WIN_TOK, :] = main.astype(jnp.int32)
        rest = dot(dot(to_q_rest_ref[...], values).astype(jnp.bfloat16), to_k_rest_ref[...])
        rest = jnp.where(rest_lane == rest_row, rest, 0.0).astype(jnp.bfloat16)
        rest = dot(gather, rest).astype(jnp.int32)
        ref[WIN_TOK : WIN_TOK + 16, :] = rest[:, 0:128]
        ref[WIN_TOK + 16 : WIN_TOK + 32, :] = rest[:, 128:256]


def stack_tables(before_ref, own_ref, table_ref):
    positions = own_ref.shape[-1]
    for k in range(table_ref.shape[1] // 48):
        end = min(positions, (k + 1) * LOW)
        sides = []
        for window in range(3):
            parts = []
            for zw in range(WIN_Z):
                ref = before_ref if window == 0 else own_ref.at[window - 1]
                part = ref[zw, :, k * LOW : end].astype(jnp.float32)
                if end < (k + 1) * LOW:
                    fill = jnp.zeros((part.shape[0], (k + 1) * LOW - end), jnp.float32)
                    part = jnp.concatenate([part, fill], axis=1)
                parts.append(part)
            sides.append([parts[0][:8], parts[1][:8], parts[0][8:], parts[1][8:]])
        for a, edge in ((0, 2), (1, 0)):
            block = jnp.concatenate(sides[edge] + sides[1], axis=0)
            table_ref[a, k * 48 : (k + 1) * 48, :] = block.astype(jnp.bfloat16)


def look_up_bias(a, lat, pad_ref, geometry_ref, low_ref, high_ref, table_ref, bias_ref):
    highs = table_ref.shape[1] // 48
    lat_total = pad_ref.shape[0]
    windows = lat_total // WIN_LAT
    half_row = iota((8, LOW), 0) < 4
    low_iota = iota((LOW, LOW), 0)

    def look_up(tile, low, high):
        hot = jnp.where(low_iota == low, 1.0, 0.0).astype(jnp.bfloat16)
        found = dot(table_ref[a], hot)
        high = jnp.broadcast_to(high, (8, LOW))
        total = [found[8 * j : 8 * j + 8] for j in range(6)]
        for k in range(1, highs):
            here = high == k
            for j in range(6):
                row = k * 48 + 8 * j
                total[j] = jnp.where(here, found[row : row + 8], total[j])
        geometry = geometry_ref[tile]
        key_row, same_half, same_level = geometry[0:1], geometry[1:2], geometry[2:3]
        pieces = []
        for s in range(2):
            window = 2 * lat
            if s == 0:
                window = lax.rem(2 * lat - 1 + windows if a == 1 else 2 * lat + 1, windows)
            usable = jnp.zeros((1, LOW), jnp.int32)
            for n in range(WIN_LAT):
                source = lax.rem(window * WIN_LAT + n + HALF_LAT, lat_total)
                usable = jnp.where(key_row == n, pad_ref[source], usable)
            inner = (window != windows - 1).astype(jnp.int32)
            usable = jnp.where(usable == 1, jnp.maximum(same_half, inner), 0)
            first = jnp.broadcast_to(usable, (8, LOW))
            second = jnp.broadcast_to(usable * same_level, (8, LOW))
            for kind, allowed in enumerate((first, second, jnp.where(half_row, first, second))):
                pieces.append(jnp.where(allowed == 1, total[s * 3 + kind], SHUT))
        return pieces

    def pair(p, carry):
        tile = a * 36 + p

        def two(ref):
            return jnp.concatenate(
                [ref[pl.ds(2 * tile, 1), :], ref[pl.ds(2 * tile + 1, 1), :]], axis=1
            )

        pieces = look_up(tile, two(low_ref), two(high_ref))
        for s in range(2):
            for kind in range(3):
                part = pieces[s * 3 + kind]
                bias_ref[a, s, kind, 2 * p, :, 0:128] = part[:, 0:128]
                bias_ref[a, s, kind, 2 * p + 1, :, 0:128] = part[:, 128:256]
        return carry

    lax.fori_loop(0, 36, pair, 0, unroll=2)
    for tile in range(5):
        row = WIN_TOK + a * 5 + tile

        def wide(ref, row=row):
            return jnp.concatenate([ref[row : row + 1, :], ref[row + 16 : row + 17, :]], axis=1)

        pieces = look_up(72 + a * 5 + tile, wide(low_ref), wide(high_ref))
        for j in range(16):
            q = tile * 16 + j
            if q < 72:
                for s in range(2):
                    for kind in range(3):
                        part = pieces[s * 3 + kind]
                        bias_ref[a, s, kind, q, :, 128:144] = part[:, 16 * j : 16 * j + 16]


def layer_kernel(
    state_hbm,
    w_qkv_hbm,
    w_proj_hbm,
    table_own_ref,
    index_ref,
    pad_ref,
    land_mask_ref,
    land_embed_ref,
    offset_ref,
    gain_ref,
    shift_ref,
    pick_ref,
    restore_ref,
    to_q_ref,
    to_k_ref,
    to_q_rest_ref,
    to_k_rest_ref,
    geometry_ref,
    out_ref,
    state_ref,
    w_qkv_ref,
    w_proj_ref,
    before_ref,
    hidden_ref,
    tokens_ref,
    from_lon_ref,
    from_lat_ref,
    queries_ref,
    keys_ref,
    tails_ref,
    low_ref,
    high_ref,
    table_ref,
    bias_ref,
    attended_ref,
    local_sem,
    send_sem,
    recv_sem,
    table_sem,
    lat_send_sem,
    lat_recv_sem,
):
    lat = lax.axis_index("lat")
    lon = lax.axis_index("lon")
    lon_count = lax.axis_size("lon")
    other = 1 - lat
    left = lax.rem(lon + lon_count - 1, lon_count)
    right = lax.rem(lon + 1, lon_count)
    loads = [
        pltpu.make_async_copy(source, target, local_sem.at[n])
        for n, (source, target) in enumerate(
            ((state_hbm, state_ref), (w_qkv_hbm, w_qkv_ref), (w_proj_hbm, w_proj_ref))
        )
    ]
    for load in loads:
        load.start()
    barrier = pltpu.get_barrier_semaphore()
    for device in ({"lon": left}, {"lon": right}, {"lat": other}):
        pl.semaphore_signal(barrier, inc=1, device_id=device, device_id_type=MESH)

    levels, lat_rows, lon_columns, features = state_ref.shape
    hidden_ref[:, :, 8:16, :] = jnp.zeros((levels, lat_rows, 8, features), jnp.bfloat16)
    loads[0].wait()

    eye = iota((lon_columns, lon_columns), 0) == iota((lon_columns, lon_columns), 1)

    def embed(i, carry):
        row = jnp.broadcast_to(land_mask_ref[pl.ds(i, 1), :], (lon_columns, lon_columns))
        row = jnp.where(eye, row.astype(jnp.float32), 0.0)
        land = jnp.sum(row, axis=1, keepdims=True) > 0.5
        embedded = jnp.where(land, land_embed_ref[1:2, :], land_embed_ref[0:1, :])
        for z in range(levels):
            hidden = state_ref[z, i].astype(jnp.float32) + embedded
            hidden_ref[z, i, 0:lon_columns, :] = hidden.astype(jnp.bfloat16)
        return carry

    lax.fori_loop(0, lat_rows, embed, 0)

    edge = 3 * other
    wrap = 3 * lat
    quarters = (edge, wrap, 1, 2)
    halves = (lat, other, 0, 1)

    def group(quarter):
        rows = [
            hidden_ref[z, pl.ds(quarter * HALF_LAT, HALF_LAT)].reshape(SLOT, features)
            for z in range(levels)
        ]
        return dot(pick_ref[...], jnp.concatenate(rows, axis=0))

    def group_pair(n):
        first, second = group(quarters[2 * n]), group(quarters[2 * n + 1])
        for side in range(2):
            part = slice(side * PAIR, (side + 1) * PAIR)
            both = jnp.concatenate([first[part], second[part]], axis=0)
            tokens_ref[side, 2 * n * PAIR : 2 * (n + 1) * PAIR] = both.astype(jnp.bfloat16)

    pieces = ((0, 80), (144, 80), (224, 64), (80, 64))

    def lon_copy(side, n):
        start, size = pieces[n]
        return pltpu.make_async_remote_copy(
            src_ref=tokens_ref.at[side, pl.ds(start, size)],
            dst_ref=from_lon_ref.at[1 - side, pl.ds(start, size)],
            send_sem=send_sem.at[side, n],
            recv_sem=recv_sem.at[1 - side, n],
            device_id={"lon": right if side == 1 else left},
            device_id_type=MESH,
        )

    def lat_copy(column):
        source = tokens_ref.at[column - 1] if column in (1, 2) else from_lon_ref.at[column // 3]
        return pltpu.make_async_remote_copy(
            src_ref=source.at[pl.ds(0, EDGE_ROWS)],
            dst_ref=from_lat_ref.at[column],
            send_sem=lat_send_sem.at[column],
            recv_sem=lat_recv_sem.at[column],
            device_id={"lat": other},
            device_id_type=MESH,
        )

    table_copy = pltpu.make_async_remote_copy(
        src_ref=table_own_ref.at[1],
        dst_ref=before_ref,
        send_sem=table_sem.at[0],
        recv_sem=table_sem.at[1],
        device_id={"lat": other},
        device_id_type=MESH,
    )

    group_pair(0)
    pl.semaphore_wait(barrier, 3)
    for side in (1, 0):
        lon_copy(side, 0).start()
    table_copy.start()
    group_pair(1)
    for n in range(1, 4):
        for side in (1, 0):
            lon_copy(side, n).start()
    for column in (1, 2):
        lat_copy(column).start()

    def place(values, window, side, a, b):
        row = pl.multiple_of(32 * (2 * a + b), 32)
        for zw in range(2):
            part = values[32 * zw : 32 * zw + 32].astype(jnp.bfloat16)
            keys_ref[window, side, zw, pl.ds(row, 32), :] = part
        tails_ref[window, side, 2 * a + b] = values[64:72]

    def place_pair(values, n, side, b):
        for m in range(2):
            slot = 2 * n + m
            place(values[m * PAIR : (m + 1) * PAIR], min(slot, 2), side, halves[slot], b)

    lower = iota((8, 2 * WIDTH), 0) < 4

    def place_tails(window, side):
        t = [tails_ref[window, side, n] for n in range(4)]
        for zw in range(2):
            rows = []
            for n in (0, 2):
                x, y = t[n], t[n + 1]
                if zw == 0:
                    y = pltpu.roll(y, 4, 0)
                else:
                    x = pltpu.roll(x, 4, 0)
                rows.append(jnp.where(lower, x, y))
            keys_ref[window, side, zw, 128:144, :] = jnp.concatenate(rows, axis=0).astype(
                jnp.bfloat16
            )

    index_planes(
        index_ref, to_q_ref, to_k_ref, to_q_rest_ref, to_k_rest_ref, low_ref, high_ref
    )
    for side in range(2):
        empty = pl.multiple_of(64 * lat, 64)
        for zw in range(2):
            keys_ref[1, side, zw, pl.ds(empty, 64), :] = jnp.zeros((64, 2 * WIDTH), jnp.bfloat16)
        for b in range(2):
            tails_ref[1, side, 2 * lat + b] = jnp.zeros((8, 2 * WIDTH), jnp.float32)

    loads[1].wait()
    for side in range(2):
        for n in range(2):
            tokens = tokens_ref[side, 2 * n * PAIR : 2 * (n + 1) * PAIR]
            qkv = dot(tokens, w_qkv_ref[...])
            for m in range(2):
                part = qkv[m * PAIR : (m + 1) * PAIR, 0:WIDTH]
                for zw in range(2):
                    main = part[32 * zw : 32 * zw + 32].astype(jnp.bfloat16)
                    tail = part[64 + 4 * zw : 68 + 4 * zw].astype(jnp.bfloat16)
                    queries_ref[side, 2 * n + m, zw, 0:32] = main
                    queries_ref[side, 2 * n + m, zw, 32:36] = tail
            place_pair(qkv[:, WIDTH:], n, side, 1 - side)

    table_copy.wait()
    stack_tables(before_ref, table_own_ref, table_ref)
    look_up_bias(0, lat, pad_ref, geometry_ref, low_ref, high_ref, table_ref, bias_ref)
    for side in range(2):
        lon_copy(1 - side, 0).wait_recv()
    for column in (0, 3):
        lat_copy(column).start()
    look_up_bias(1, lat, pad_ref, geometry_ref, low_ref, high_ref, table_ref, bias_ref)

    def project(tokens):
        return dot(tokens, w_qkv_ref[:, WIDTH : 3 * WIDTH])

    for column in range(4):
        lat_copy(column).wait_recv()
        values = project(from_lat_ref[column])
        place(values, 0, column // 2, other, column % 2)
    for n in (1, 2, 3):
        for side in range(2):
            lon_copy(1 - side, n).wait_recv()
    for n in (0, 1):
        for side in range(2):
            values = project(from_lon_ref[side, 2 * n * PAIR : 2 * (n + 1) * PAIR])
            place_pair(values, n, side, side)
    for window in range(3):
        for side in range(2):
            place_tails(window, side)

    head_mask = jnp.where(iota((8, 256), 1) // HEAD_DIM == iota((8, 256), 0), 1.0, 0.0)
    gather_rows = jnp.where(
        iota((SLOT, 8 * GROUP), 1) // 8 == iota((SLOT, 8 * GROUP), 0), 1.0, 0.0
    ).astype(jnp.bfloat16)

    def attend(step, carry):
        slot, side = step // 2, lax.rem(step, 2)
        window = jnp.minimum(slot, 2)
        a = jnp.where(slot == 0, lat, jnp.where(slot == 1, other, slot - 2))
        edge_kind = jnp.where(slot < 2, 0, 1)
        first = pl.multiple_of((1 - side) * GROUP, GROUP)
        results = []
        for kind in range(3):
            if kind < 2:
                q = queries_ref[side, slot, kind, :, 0:256]
                key = keys_ref[window, side, kind, :, 0:256]
                value = keys_ref[window, side, kind, :, WIDTH : WIDTH + 256]
            else:
                q, key, value = (
                    jnp.concatenate([ref[0, :, n : n + 128], ref[1, :, n : n + 128]], axis=1)
                    for ref, n in (
                        (queries_ref.at[side, slot], 256),
                        (keys_ref.at[window, side], 256),
                        (keys_ref.at[window, side], 640),
                    )
                )
            q = q.astype(jnp.float32)[0:GROUP]
            spread = (q[:, None, :] * head_mask[None]).reshape(8 * GROUP, 256)
            scores = lax.dot_general(
                spread.astype(jnp.bfloat16),
                key,
                (((1,), (1,)), ((), ())),
                preferred_element_type=jnp.float32,
            )
            bias = bias_ref[a, edge_kind, kind, pl.ds(first, GROUP)]
            bias = bias.reshape(8 * GROUP, 256)[:, 0:WIN_TOK]
            scores = scores * (HEAD_DIM**-0.5) + bias
            powers = jnp.exp(scores - jnp.max(scores, axis=-1, keepdims=True))
            weights = (powers / jnp.sum(powers, axis=-1, keepdims=True)).astype(jnp.bfloat16)
            mixed = dot(weights, value)
            mixed = (mixed.reshape(GROUP, 8, 256) * head_mask[None]).reshape(8 * GROUP, 256)
            results.append(dot(gather_rows, mixed.astype(jnp.bfloat16)).astype(jnp.bfloat16))
        for zw in range(2):
            row = pl.multiple_of((side * 2 + zw) * SLOT, SLOT)
            attended_ref[slot, pl.ds(row, SLOT), 0:256] = results[zw]
            attended_ref[slot, pl.ds(row, SLOT), 256:384] = results[2][
                :, zw * 128 : zw * 128 + 128
            ]
        return carry

    lax.fori_loop(0, 8, attend, 0)
    loads[2].wait()

    def finish(slot, carry):
        quarter = jnp.where(slot == 0, edge, jnp.where(slot == 1, wrap, slot - 1))
        natural = dot(restore_ref[...], attended_ref[slot]).astype(jnp.bfloat16)
        projected = dot(natural, w_proj_ref[...]) + offset_ref[...]
        centered = projected - jnp.mean(projected, axis=-1, keepdims=True)
        spread = jnp.mean(centered * centered, axis=-1, keepdims=True)
        normed = centered * lax.rsqrt(spread + norm_epsilon) * gain_ref[...] + shift_ref[...]
        normed = normed.reshape(levels, HALF_LAT, 16, features)
        rows = pl.ds(quarter * HALF_LAT, HALF_LAT)
        hidden = hidden_ref[:, rows].astype(jnp.float32)
        result = (hidden + normed).astype(jnp.bfloat16)
        out_ref[:, rows] = result[:, :, 0:lon_columns, :]
        return carry

    lax.fori_loop(0, 4, finish, 0)

    table_copy_done = table_copy
    for side in range(2):
        for n in range(4):
            lon_copy(side, n).wait_send()
    for column in range(4):
        lat_copy(column).wait_send()


def as_tiles(rows):
    main = rows[:, :128].reshape(72, 256)
    rest = np.pad(rows[:, 128:].reshape(2, 72, 16), ((0, 0), (0, 8), (0, 0))).reshape(10, 256)
    return np.concatenate([main, rest], axis=0)


def bias_constants():
    queries, keys = window_orders()
    eye = np.eye(WIN_TOK, dtype=np.float32)
    to_q = eye[queries]
    to_q_rest = np.pad(to_q.reshape(2, 72, WIN_TOK), ((0, 0), (0, 8), (0, 0)))
    to_q_rest = to_q_rest.reshape(160, WIN_TOK)
    to_k = eye[keys[:128]].T
    to_k_rest = eye[np.tile(keys[128:], 16)].T
    q_level, q_half = queries // 72, queries // 12 % 6 // 3
    k_level, k_row = keys // 72, keys // 12 % 6
    planes = [
        np.broadcast_to(k_row[None, :], (WIN_TOK, WIN_TOK)),
        q_half[:, None] == (k_row // 3)[None, :],
        q_level[:, None] == k_level[None, :],
    ]
    geometry = np.stack([as_tiles(p.astype(np.int32)) for p in planes], axis=1)
    matrices = [jnp.asarray(m, jnp.bfloat16) for m in (to_q, to_k, to_q_rest, to_k_rest)]
    return matrices + [jnp.asarray(geometry)]


def group_constants(levels, columns):
    pick = np.zeros((2 * PAIR, levels * SLOT), np.float32)
    restore = np.zeros((levels * SLOT, 2 * WIN_Z * SLOT), np.float32)
    for side in range(2):
        for zw in range(WIN_Z):
            for t in range(GROUP):
                dz, rest = divmod(t, HALF_LAT * HALF_LON)
                di, dj = divmod(rest, HALF_LON)
                z = (WIN_Z * zw + dz + WIN_Z // 2) % levels
                natural = (z * HALF_LAT + di) * 16 + side * HALF_LON + dj
                place = 32 * zw + t if t < 32 else 64 + 4 * zw + t - 32
                pick[side * PAIR + place, natural] = 1.0
                restore[natural, (side * WIN_Z + zw) * SLOT + t] = 1.0
    return jnp.asarray(pick, jnp.bfloat16), jnp.asarray(restore, jnp.bfloat16)


def on_device(
    state_tokens,
    land_mask,
    pad_mask,
    land_embed,
    w_qkv,
    w_proj,
    proj_bias,
    norm_gain,
    norm_shift,
    bias_table,
    index_table,
):
    levels, lat_rows, lon_columns, features = state_tokens.shape
    assert (levels, lat_rows, lon_columns) == (2 * WIN_Z, 2 * WIN_LAT, WIN_LON)
    assert lax.axis_size("lat") == 2 and lax.axis_size("lon") > 2
    highs = -(-bias_table.shape[-1] // LOW)
    vectors = [v.reshape(1, features) for v in (proj_bias, norm_gain, norm_shift)]
    constants = [*group_constants(levels, lon_columns), *bias_constants()]
    hbm = pl.BlockSpec(memory_space=pl.ANY)
    vmem = pl.BlockSpec(memory_space=pltpu.VMEM)
    smem = pl.BlockSpec(memory_space=pltpu.SMEM)
    bf16, f32, i32 = jnp.bfloat16, jnp.float32, jnp.int32
    dma = pltpu.SemaphoreType.DMA
    return pl.pallas_call(
        layer_kernel,
        out_shape=jax.ShapeDtypeStruct(state_tokens.shape, bf16),
        in_specs=[hbm] * 3 + [vmem] * 2 + [smem] + [vmem] * 12,
        out_specs=vmem,
        scratch_shapes=[
            pltpu.VMEM(state_tokens.shape, bf16),
            pltpu.VMEM(w_qkv.shape, bf16),
            pltpu.VMEM(w_proj.shape, bf16),
            pltpu.VMEM(bias_table.shape[1:], bf16),
            pltpu.VMEM((levels, lat_rows, 16, features), bf16),
            pltpu.VMEM((2, 4 * PAIR, features), bf16),
            pltpu.VMEM((2, 4 * PAIR, features), bf16),
            pltpu.VMEM((4, EDGE_ROWS, features), bf16),
            pltpu.VMEM((2, 4, WIN_Z, SLOT, WIDTH), bf16),
            pltpu.VMEM((3, 2, WIN_Z, WIN_TOK, 2 * WIDTH), bf16),
            pltpu.VMEM((3, 2, 4, 8, 2 * WIDTH), f32),
            pltpu.VMEM((WIN_TOK + 32, 128), i32),
            pltpu.VMEM((WIN_TOK + 32, 128), i32),
            pltpu.VMEM((2, highs * 48, LOW), bf16),
            pltpu.VMEM((2, 2, 3, 2 * GROUP, 8, 256), f32),
            pltpu.VMEM((4, 4 * SLOT, WIDTH), bf16),
            dma((3,)),
            dma((2, 4)),
            dma((2, 4)),
            dma((2,)),
            dma((4,)),
            dma((4,)),
        ],
        compiler_params=pltpu.CompilerParams(
            collective_id=0, has_side_effects=True, vmem_limit_bytes=56 << 20
        ),
        name="layer",
    )(
        state_tokens,
        w_qkv,
        w_proj,
        bias_table,
        index_table,
        pad_mask,
        land_mask,
        land_embed,
        *vectors,
        *constants,
    )


def solution(mesh):
    in_specs = (
        P("member", "lat", "lon", None),
        P("lat", "lon"),
        P(),
        P(),
        P(),
        P(),
        P(),
        P(),
        P(),
        P("lat", None, None, None),
        P(),
    )
    out_specs = P("member", "lat", "lon", None)
    return jax.shard_map(
        on_device, mesh=mesh, in_specs=in_specs, out_specs=out_specs, check_vma=False
    )
```

time: 81.9 us -> 55.5 us (0.68)
  waiting for transfers between devices: 20.3 us -> 0 us
  Pallas kernels: 37.1 us -> 44.4 us
  starting transfers between devices: 6.68 us -> 0 us
  matrix products: 4.04 us -> 0 us
  other arithmetic: 3.13 us -> 0 us
  local copies, waits for them, and re-layouts: 9.26 us -> 10.8 us
    ppermute x5 -> x0, waiting for transfers between devices: 20.3 us -> none  [from_behind(): lax.ppermute(shard, axis, [(i, (i + by) % size) for i in range(size)])]
    pallas_call x2 -> x1, Pallas kernels: 37.1 us -> 44.4 us  [on_device(): pl.pallas_call(layer_kernel, out_shape=jax.ShapeDtypeStruct(state_tokens....]
    ppermute x5 -> x0, starting transfers between devices: 6.68 us -> none  [from_behind(): lax.ppermute(shard, axis, [(i, (i + by) % size) for i in range(size)])]
    dot_general x1 -> x0, matrix products: 4.04 us -> none  [on_device(): qkv = jnp.dot(grouped, w_qkv, preferred_element_type=jnp.float32)]
    reshape x3, local copies, waits for them, and re-layouts: 0.01 us -> 3.84 us  [on_device(): v.reshape(1, features)]
    unnamed x46 -> x2, local copies, waits for them, and re-layouts: 1.05 us -> 4.08 us
    pallas_call x0 -> x1, local copies, waits for them, and re-layouts: none -> 2.87 us  [on_device(): pl.pallas_call(layer_kernel, out_shape=jax.ShapeDtypeStruct(state_tokens....]
    slice x3 -> x0, local copies, waits for them, and re-layouts: 2.79 us -> none  [the longest x1 1 us: on_device(): left[0]]
  transfers between devices with their start and end apart: 5 -> 0, of which waited for: 1 -> 0; matrix products, arithmetic and copies ran while one was open for 5% -> 0% of each run, Pallas kernels for 27% -> 0%
where the time goes in v1:
time: 55.5 us; the launch traced here: 55.2 us
  Pallas kernels  44.4 us (80%)
  local copies, waits for them, and re-layouts  10.8 us (19%)
    pallas_call x1, Pallas kernels, on_device(): pl.pallas_call(layer_kernel, out_shape=jax.ShapeDtypeStruct(state_tokens....  44.4 us
    unnamed x2, local copies, waits for them, and re-layouts  4.08 us
    reshape x3, local copies, waits for them, and re-layouts, on_device(): v.reshape(1, features)  3.84 us
    pallas_call x1, local copies, waits for them, and re-layouts, on_device(): pl.pallas_call(layer_kernel, out_shape=jax.ShapeDtypeStruct(state_tokens....  2.87 us

profile of v1, /device:TPU:0, one launch (start us, length us, event | category | flops | bytes accessed | tf_op | source)
XLA Modules:
  0.0 55.2 jit_solution(15246925889548096746)
XLA Ops:
  0.0 1.3 %reshape.9.offset_ref = f32[1,768]{1,0:T(1,128)} reshape(f32[768]{0:T(1024)} %param.24) | data formatting | bytes 6144 | tf_op jit(solution)/shard_map/reshape | solution.py:518
  1.3 1.3 %reshape.10.gain_ref = f32[1,768]{1,0:T(1,128)} reshape(f32[768]{0:T(1024)} %param.25) | data formatting | bytes 6144 | tf_op jit(solution)/shard_map/reshape | solution.py:518
  2.6 1.3 %reshape.11.shift_ref = f32[1,768]{1,0:T(1,128)} reshape(f32[768]{0:T(1024)} %param.26) | data formatting | bytes 6144 | tf_op jit(solution)/shard_map/reshape | solution.py:518
  3.8 1.8 %copy.20.table_own_ref = bf16[2,2,12,3312]{3,2,1,0:T(8,128)(2,1)} copy(bf16[2,2,12,3312]{3,1,2,0:T(2,128)(2,1)} %param.27) | data formatting | bytes 635904 | tf_op args[9]
  5.6 2.3 %copy.19.state_hbm = bf16[4,12,12,768]{3,2,1,0:T(8,128)(2,1)} copy(bf16[4,12,12,768]{3,0,2,1:T(4,128)(2,1)} %param.18) | data formatting | bytes 1769472 | tf_op args[0]
  7.9 44.4 %layer.1 = bf16[4,12,12,768]{3,2,1,0:T(8,128)(2,1)} custom-call(bf16[4,12,12,768]{3,2,1,0:T(8,128)(2,1)} %copy.19.state_hbm, bf16[768,1152]{1,0:T(8,128)(2,1)} %w_qkv_hbm.1, bf16[384,768]{1,0:T(8,128)(2,1)} %w_proj_hbm.1, bf16[2,2,12,3312]{3,2,1,0:T(8,128)(2,1)} %copy.20.table_own_ref, s32[144,144]{1,0:T(8,128)} %index_ref.1, s32[24]{0:T(128)} %pad_ref.1, ...), custom_call_target="tpu_custom_call" | custom-call | tf_op jit(solution)/shard_map/layer/pallas_call | solution.py:525
  52.3 2.9 %copy.21 = bf16[4,12,12,768]{3,0,2,1:T(4,128)(2,1)} copy(bf16[4,12,12,768]{3,2,1,0:T(8,128)(2,1)} %layer.1) | data formatting | bytes 1769472 | tf_op jit(solution)/shard_map/layer/pallas_call | solution.py:525

commit v2 on v1

v2 whole, which is shorter than its diff:
```python
import functools

import jax
import jax.numpy as jnp
import numpy as np
from jax import lax
from jax.experimental import pallas as pl
from jax.experimental.pallas import tpu as pltpu
from jax.sharding import PartitionSpec as P

HEADS = 12
HEAD_DIM = 32
WIN_Z = 2
WIN_LAT = 6
WIN_LON = 12
WIN_TOK = 144
HALF_LAT = WIN_LAT // 2
HALF_LON = WIN_LON // 2
GROUP = WIN_Z * HALF_LAT * HALF_LON
PAIR = WIN_Z * GROUP
SLOT = 48
BLOCK = 48
EDGE_ROWS = 80
LOW = 256
SHUT = -1e30
LOG2E = 1.4426950408889634
WIDTH = HEADS * HEAD_DIM
MESH = pl.DeviceIdType.MESH

norm_epsilon = 1e-05


def group_tokens(a, b):
    dz, di, dj = np.meshgrid(
        np.arange(WIN_Z), np.arange(HALF_LAT), np.arange(HALF_LON), indexing="ij"
    )
    return ((dz * WIN_LAT + a * HALF_LAT + di) * WIN_LON + b * HALF_LON + dj).reshape(-1)


def window_orders():
    groups = [group_tokens(a, b) for a in range(2) for b in range(2)]
    queries = np.concatenate(groups)
    keys = np.concatenate([g[:32] for g in groups] + [g[32:] for g in groups])
    return queries, keys


def dot(x, y):
    return jnp.dot(x, y, preferred_element_type=jnp.float32)


def iota(shape, axis):
    return lax.broadcasted_iota(jnp.int32, shape, axis)


def index_planes(index_ref, to_q_ref, to_k_ref, to_q_rest_ref, to_k_rest_ref, low_ref, high_ref):
    index = index_ref[...]
    rest_lane = iota((160, LOW), 1) // 16
    rest_row = iota((160, LOW), 0) % 16
    gather = jnp.where(iota((16, 160), 1) // 16 == iota((16, 160), 0), 1.0, 0.0)
    gather = gather.astype(jnp.bfloat16)
    for values, ref in ((index % LOW, low_ref), (index // LOW, high_ref)):
        values = values.astype(jnp.float32).astype(jnp.bfloat16)
        main = dot(dot(to_q_ref[...], values).astype(jnp.bfloat16), to_k_ref[...])
        ref[0:WIN_TOK, :] = main.astype(jnp.int32)
        rest = dot(dot(to_q_rest_ref[...], values).astype(jnp.bfloat16), to_k_rest_ref[...])
        rest = jnp.where(rest_lane == rest_row, rest, 0.0).astype(jnp.bfloat16)
        rest = dot(gather, rest).astype(jnp.int32)
        ref[WIN_TOK : WIN_TOK + 16, :] = rest[:, 0:128]
        ref[WIN_TOK + 16 : WIN_TOK + 32, :] = rest[:, 128:256]


def stack_tables(before_ref, own_ref, rows_ref, table_ref):
    positions = own_ref.shape[-1]
    heads = own_ref.shape[1]
    for window in range(3):
        ref = before_ref if window == 0 else own_ref.at[window - 1]
        for k in range(table_ref.shape[1] // BLOCK):
            end = min(positions, (k + 1) * LOW)
            for h in range(heads):
                part = ref[h, :, k * LOW : end].astype(jnp.float32)
                if end < (k + 1) * LOW:
                    fill = jnp.zeros((WIN_Z, (k + 1) * LOW - end), jnp.float32)
                    part = jnp.concatenate([part, fill], axis=1)
                row = (k * heads + h) * WIN_Z
                rows_ref[window, row : row + WIN_Z, :] = part
    size = heads * WIN_Z
    for k in range(table_ref.shape[1] // BLOCK):
        own = rows_ref[1, k * size : (k + 1) * size]
        for a, edge in ((0, 2), (1, 0)):
            block = jnp.concatenate([rows_ref[edge, k * size : (k + 1) * size], own], axis=0)
            table_ref[a, k * BLOCK : (k + 1) * BLOCK, :] = block.astype(jnp.bfloat16)


def look_up_bias(a, closed, pad_ref, geometry_ref, low_ref, high_ref, table_ref, bias_ref, halfway):
    highs = table_ref.shape[1] // BLOCK
    lat_total = pad_ref.shape[0]
    odd_row = iota((8, LOW), 0) % 2 == 1
    low_iota = iota((LOW, LOW), 0)

    def look_up(tile, low, high):
        hot = jnp.where(low_iota == low, 1.0, 0.0).astype(jnp.bfloat16)
        found = dot(table_ref[a], hot)
        high = jnp.broadcast_to(high, (8, LOW))
        total = [found[8 * j : 8 * j + 8] for j in range(6)]
        for k in range(1, highs):
            here = high == k
            for j in range(6):
                row = k * BLOCK + 8 * j
                total[j] = jnp.where(here, found[row : row + 8], total[j])
        geometry = geometry_ref[tile]
        key_row, same_half, same_level = geometry[0:1], geometry[1:2], geometry[2:3]
        levels = jnp.where(odd_row, jnp.broadcast_to(same_level, (8, LOW)), 1)
        allowed = [levels, levels]
        if closed:
            usable = jnp.zeros((1, LOW), jnp.int32)
            for n in range(WIN_LAT):
                source = (lat_total - HALF_LAT + n) % lat_total
                usable = jnp.where(key_row == n, pad_ref[source], usable)
            usable = jnp.where(usable == 1, same_half, 0)
            allowed[0] = levels * jnp.broadcast_to(usable, (8, LOW))
        return [
            jnp.where(allowed[s] == 1, total[s * 3 + kind] * LOG2E, SHUT)
            for s in range(2)
            for kind in range(3)
        ]

    def pair(p, carry):
        tile = a * 36 + p

        def two(ref):
            return jnp.concatenate(
                [ref[pl.ds(2 * tile, 1), :], ref[pl.ds(2 * tile + 1, 1), :]], axis=1
            )

        pieces = look_up(tile, two(low_ref), two(high_ref))
        for s in range(2):
            for kind in range(3):
                part = pieces[s * 3 + kind]
                bias_ref[a, s, kind, 2 * p, :, 0:128] = part[:, 0:128]
                bias_ref[a, s, kind, 2 * p + 1, :, 0:128] = part[:, 128:256]
        return carry

    lax.fori_loop(0, 20, pair, 0, unroll=4)
    halfway()
    lax.fori_loop(20, 36, pair, 0, unroll=4)
    for tile in range(5):
        row = WIN_TOK + a * 5 + tile

        def wide(ref, row=row):
            return jnp.concatenate([ref[pl.ds(row, 1), :], ref[pl.ds(row + 16, 1), :]], axis=1)

        pieces = look_up(72 + a * 5 + tile, wide(low_ref), wide(high_ref))
        for j in range(16):
            q = tile * 16 + j
            if q < 72:
                for s in range(2):
                    for kind in range(3):
                        part = pieces[s * 3 + kind]
                        bias_ref[a, s, kind, q, :, 128:144] = part[:, 16 * j : 16 * j + 16]


def layer_kernel(*refs):
    inputs, refs = refs[:18], refs[18:]
    out_hbm, refs = refs[0], refs[1:]
    copies, refs = refs[:18], refs[18:]
    (
        before_ref,
        hidden_ref,
        tokens_ref,
        from_lon_ref,
        from_lat_ref,
        queries_ref,
        keys_ref,
        tails_ref,
        low_ref,
        high_ref,
        rows_ref,
        table_ref,
        bias_ref,
        attended_ref,
        result_ref,
        local_sem,
        out_sem,
        send_sem,
        recv_sem,
        table_sem,
        lat_send_sem,
        lat_recv_sem,
    ) = refs
    lat = lax.axis_index("lat")
    lon = lax.axis_index("lon")
    lon_count = lax.axis_size("lon")
    other = 1 - lat
    left = lax.rem(lon + lon_count - 1, lon_count)
    right = lax.rem(lon + 1, lon_count)
    loads = [
        pltpu.make_async_copy(source, target, local_sem.at[n])
        for n, (source, target) in enumerate(zip(inputs, copies))
    ]
    for load in loads:
        load.start()
    (
        state_ref,
        land_mask_ref,
        land_embed_ref,
        pick_ref,
        w_qkv_ref,
        table_own_ref,
        index_ref,
        to_q_ref,
        to_k_ref,
        to_q_rest_ref,
        to_k_rest_ref,
        geometry_ref,
        pad_ref,
        w_proj_ref,
        offset_ref,
        gain_ref,
        shift_ref,
        restore_ref,
    ) = copies
    barrier = pltpu.get_barrier_semaphore()
    for device in ({"lon": left}, {"lon": right}, {"lat": other}):
        pl.semaphore_signal(barrier, inc=1, device_id=device, device_id_type=MESH)

    lat_rows, lon_columns, levels, features = state_ref.shape
    strip = lon_columns * levels
    part_rows = HALF_LAT * strip
    with jax.named_scope("wait_state"):
        for n in (1, 2, 0):
            loads[n].wait()

    def embed(i, carry):
        sea, land = (
            jnp.broadcast_to(land_embed_ref[n : n + 1, :], (levels, features)) for n in range(2)
        )
        rows = []
        for j in range(lon_columns):
            embedded = jnp.where(land_mask_ref[i, j] == 1, land, sea)
            rows.append(state_ref[i, j].astype(jnp.float32) + embedded)
        hidden = jnp.concatenate(rows, axis=0).astype(jnp.bfloat16).astype(jnp.float32)
        hidden_ref[pl.ds(pl.multiple_of(i * strip, strip), strip), :] = hidden
        return carry

    with jax.named_scope("embed"):
        lax.fori_loop(0, lat_rows, embed, 0)

    edge = 3 * other
    wrap = 3 * lat
    quarters = (edge, wrap, 1, 2)
    halves = (lat, other, 0, 1)
    loads[3].wait()

    def natural_rows(quarter):
        return pl.ds(pl.multiple_of(quarter * part_rows, 16), part_rows)

    def group(quarter):
        return dot(pick_ref[...], hidden_ref[natural_rows(quarter)].astype(jnp.bfloat16))

    def group_pair(n):
        first, second = group(quarters[2 * n]), group(quarters[2 * n + 1])
        for side in range(2):
            part = slice(side * PAIR, (side + 1) * PAIR)
            both = jnp.concatenate([first[part], second[part]], axis=0)
            tokens_ref[side, 2 * n * PAIR : 2 * (n + 1) * PAIR] = both.astype(jnp.bfloat16)

    pieces = ((0, 80), (144, 80), (224, 64), (80, 64))

    far = lax.rem(lon, 2)
    near = 1 - far

    def lon_copy(side, n):
        start, size = pieces[n]
        return pltpu.make_async_remote_copy(
            src_ref=tokens_ref.at[side, pl.ds(start, size)],
            dst_ref=from_lon_ref.at[1 - side, pl.ds(start, size)],
            send_sem=send_sem.at[side, n],
            recv_sem=recv_sem.at[1 - side, n],
            device_id={"lon": jnp.where(side == 1, right, left)},
            device_id_type=MESH,
        )

    def lat_copy(column):
        source = tokens_ref.at[column - 1] if column in (1, 2) else from_lon_ref.at[column // 3]
        return pltpu.make_async_remote_copy(
            src_ref=source.at[pl.ds(0, EDGE_ROWS)],
            dst_ref=from_lat_ref.at[column],
            send_sem=lat_send_sem.at[column],
            recv_sem=lat_recv_sem.at[column],
            device_id={"lat": other},
            device_id_type=MESH,
        )

    table_copy = pltpu.make_async_remote_copy(
        src_ref=table_own_ref.at[1],
        dst_ref=before_ref,
        send_sem=table_sem.at[0],
        recv_sem=table_sem.at[1],
        device_id={"lat": other},
        device_id_type=MESH,
    )

    with jax.named_scope("group0"):
        group_pair(0)
    with jax.named_scope("group1"):
        group_pair(1)

    def place(values, window, side, a, b):
        row = pl.multiple_of(32 * (2 * a + b), 32)
        for zw in range(2):
            part = values[32 * zw : 32 * zw + 32].astype(jnp.bfloat16)
            for n in range(6):
                keys_ref[window, side, n, pl.ds(row, 32), 128 * zw : 128 * zw + 128] = part[
                    :, 128 * n : 128 * n + 128
                ]
        tails_ref[window, side, 2 * a + b] = values[64:72]

    lower = iota((8, 2 * WIDTH), 0) < 4

    def place_tails(window, side):
        t = [tails_ref[window, side, n] for n in range(4)]
        for zw in range(2):
            rows = []
            for n in (0, 2):
                x, y = t[n], t[n + 1]
                if zw == 0:
                    y = pltpu.roll(y, 4, 0)
                else:
                    x = pltpu.roll(x, 4, 0)
                rows.append(jnp.where(lower, x, y))
            both = jnp.concatenate(rows, axis=0).astype(jnp.bfloat16)
            for n in range(6):
                keys_ref[window, side, n, 128:144, 128 * zw : 128 * zw + 128] = both[
                    :, 128 * n : 128 * n + 128
                ]

    with jax.named_scope("planes"):
        for n in range(6, 13):
            loads[n].wait()
        index_planes(
            index_ref, to_q_ref, to_k_ref, to_q_rest_ref, to_k_rest_ref, low_ref, high_ref
        )
    for side in range(2):
        empty = pl.multiple_of(64 * lat, 64)
        for n in range(6):
            keys_ref[1, side, n, pl.ds(empty, 64), :] = jnp.zeros((64, 256), jnp.bfloat16)
        for b in range(2):
            tails_ref[1, side, 2 * lat + b] = jnp.zeros((8, 2 * WIDTH), jnp.float32)

    with jax.named_scope("qkv"):
        loads[4].wait()
        for side in range(2):
            for n in range(2):
                tokens = tokens_ref[side, 2 * n * PAIR : 2 * (n + 1) * PAIR]
                qkv = dot(tokens, w_qkv_ref[...])
                for m in range(2):
                    slot = 2 * n + m
                    part = qkv[m * PAIR : (m + 1) * PAIR]
                    for zw in range(2):
                        main = part[32 * zw : 32 * zw + 32, 0:WIDTH].astype(jnp.bfloat16)
                        tail = part[64 + 4 * zw : 68 + 4 * zw, 0:WIDTH].astype(jnp.bfloat16)
                        for g in range(3):
                            lanes = slice(128 * g, 128 * g + 128)
                            out = slice(128 * zw, 128 * zw + 128)
                            queries_ref[side, slot, g, 0:32, out] = main[:, lanes]
                            queries_ref[side, slot, g, 32:36, out] = tail[:, lanes]
                    place(part[:, WIDTH:], min(slot, 2), side, halves[slot], 1 - side)

    loads[5].wait()
    with jax.named_scope("barrier"):
        pl.semaphore_wait(barrier, 3)
    lon_copy(far, 0).start()
    for n in range(4):
        lon_copy(near, n).start()
    table_copy.start()
    for column in (1, 2):
        lat_copy(column).start()

    with jax.named_scope("stack"):
        table_copy.wait()
        stack_tables(before_ref, table_own_ref, rows_ref, table_ref)

    def bias(a, closed, halfway):
        look_up_bias(
            a, closed, pad_ref, geometry_ref, low_ref, high_ref, table_ref, bias_ref, halfway
        )

    def forward():
        for side in range(2):
            lon_copy(1 - side, 0).wait_recv()
        for column in (0, 3):
            lat_copy(column).start()

    def project(tokens):
        return dot(tokens, w_qkv_ref[:, WIDTH : 3 * WIDTH])

    head_mask = jnp.where(
        (iota((8, 256), 1) // 128 == iota((8, 256), 0) % 2)
        & (iota((8, 256), 1) % 128 // HEAD_DIM == iota((8, 256), 0) // 2),
        1.0,
        0.0,
    )
    gather_rows = jnp.where(
        iota((SLOT, 8 * GROUP), 1) // 8 == iota((SLOT, 8 * GROUP), 0), 1.0, 0.0
    ).astype(jnp.bfloat16)

    def attend(slot, side):
        window = min(slot, 2) if isinstance(slot, int) else 2
        a = halves[slot] if isinstance(slot, int) else slot - 2
        edge_kind = 0 if isinstance(slot, int) and slot < 2 else 1
        first = (1 - side) * GROUP
        for g in range(3):
            key = keys_ref[window, side, g]
            value = keys_ref[window, side, 3 + g]
            q = queries_ref[side, slot, g].astype(jnp.float32)[0:GROUP]
            spread = (q[:, None, :] * head_mask[None]).reshape(8 * GROUP, 256)
            scores = lax.dot_general(
                spread.astype(jnp.bfloat16),
                key,
                (((1,), (1,)), ((), ())),
                preferred_element_type=jnp.float32,
            )
            bias = bias_ref[a, edge_kind, g, pl.ds(first, GROUP)]
            bias = bias.reshape(8 * GROUP, 256)[:, 0:WIN_TOK]
            scores = scores * (HEAD_DIM**-0.5 * LOG2E) + bias
            powers = jnp.exp2(scores - jnp.max(scores, axis=-1, keepdims=True))
            inverse = 1.0 / jnp.sum(powers, axis=-1, keepdims=True)
            weights = (powers * inverse).astype(jnp.bfloat16)
            mixed = dot(weights, value)
            mixed = (mixed.reshape(GROUP, 8, 256) * head_mask[None]).reshape(8 * GROUP, 256)
            part = dot(gather_rows, mixed.astype(jnp.bfloat16)).astype(jnp.bfloat16)
            for zw in range(2):
                row = (side * 2 + zw) * SLOT
                attended_ref[slot, pl.ds(row, SLOT), 128 * g : 128 * g + 128] = part[
                    :, 128 * zw : 128 * zw + 128
                ]

    def attend_sides(slot):
        for side in range(2):
            attend(slot, side)

    offset, gain, shift = offset_ref, gain_ref, shift_ref

    def out_copy(slot):
        rows = pl.ds(quarters[slot] * HALF_LAT, HALF_LAT)
        return pltpu.make_async_copy(result_ref.at[rows], out_hbm.at[rows], out_sem.at[slot])

    def finish(slot):
        quarter = quarters[slot]
        natural = dot(restore_ref[...], attended_ref[slot]).astype(jnp.bfloat16)
        projected = dot(natural, w_proj_ref[...]) + offset[...][None, :]
        centered = projected - jnp.mean(projected, axis=-1, keepdims=True)
        spread = jnp.mean(centered * centered, axis=-1, keepdims=True)
        normed = centered * lax.rsqrt(spread + norm_epsilon) * gain[...][None, :]
        normed = normed + shift[...][None, :]
        result = hidden_ref[natural_rows(quarter)] + normed
        for n in range(HALF_LAT * lon_columns):
            i, j = divmod(n, lon_columns)
            part = result[n * levels : (n + 1) * levels]
            result_ref[quarter * HALF_LAT + i, j] = part.astype(jnp.bfloat16)
        out_copy(slot).start()

    with jax.named_scope("bias_edge"):
        bias(lat, False, lambda: None)
    for n in (1, 2):
        lon_copy(far, n).start()
    with jax.named_scope("bias_wrap"):
        bias(other, True, forward)
    for n in range(13, 18):
        loads[n].wait()
    with jax.named_scope("keys_edge"):
        values = project(from_lon_ref[:, 0:EDGE_ROWS].reshape(2 * EDGE_ROWS, features))
        for side in range(2):
            place(values[EDGE_ROWS * side : EDGE_ROWS * (side + 1)], 0, side, lat, side)
        for column in range(4):
            lat_copy(column).wait_recv()
        values = project(from_lat_ref[...].reshape(4 * EDGE_ROWS, features))
        for column in range(4):
            part = values[EDGE_ROWS * column : EDGE_ROWS * (column + 1)]
            place(part, 0, column // 2, other, column % 2)
        for side in range(2):
            place_tails(0, side)
    with jax.named_scope("attend_edge"):
        attend_sides(0)
    lon_copy(far, 3).start()
    with jax.named_scope("finish_edge"):
        finish(0)
    with jax.named_scope("wait_own"):
        for n in (1, 2):
            for side in range(2):
                lon_copy(1 - side, n).wait_recv()
    with jax.named_scope("keys_own"):
        for side in range(2):
            values = project(from_lon_ref[side, 2 * PAIR : 4 * PAIR])
            for m in range(2):
                place(values[m * PAIR : (m + 1) * PAIR], 2, side, m, side)
            place_tails(2, side)
    with jax.named_scope("attend_own"):
        def own(slot, carry):
            attend_sides(slot)
            return carry

        lax.fori_loop(2, 4, own, 0)
    with jax.named_scope("finish_own"):
        finish(2)
        finish(3)
    with jax.named_scope("wait_wrap"):
        for side in range(2):
            lon_copy(1 - side, 3).wait_recv()
    with jax.named_scope("keys_wrap"):
        for side in range(2):
            values = project(from_lon_ref[side, 64 : 2 * PAIR])
            place(values[8:80], 1, side, other, side)
            place_tails(1, side)
    with jax.named_scope("attend_wrap"):
        attend_sides(1)
    with jax.named_scope("finish_wrap"):
        finish(1)
    with jax.named_scope("drain"):
        for slot in range(4):
            out_copy(slot).wait()
        for side in range(2):
            for n in range(4):
                lon_copy(side, n).wait_send()
        for column in range(4):
            lat_copy(column).wait_send()


def as_tiles(rows):
    main = rows[:, :128].reshape(72, 256)
    rest = np.pad(rows[:, 128:].reshape(2, 72, 16), ((0, 0), (0, 8), (0, 0))).reshape(10, 256)
    return np.concatenate([main, rest], axis=0)


def bias_constants():
    queries, keys = window_orders()
    eye = np.eye(WIN_TOK, dtype=np.float32)
    to_q = eye[queries]
    to_q_rest = np.pad(to_q.reshape(2, 72, WIN_TOK), ((0, 0), (0, 8), (0, 0)))
    to_q_rest = to_q_rest.reshape(160, WIN_TOK)
    to_k = eye[keys[:128]].T
    to_k_rest = eye[np.tile(keys[128:], 16)].T
    q_level, q_half = queries // 72, queries // 12 % 6 // 3
    k_level, k_row = keys // 72, keys // 12 % 6
    planes = [
        np.broadcast_to(k_row[None, :], (WIN_TOK, WIN_TOK)),
        q_half[:, None] == (k_row // 3)[None, :],
        q_level[:, None] == k_level[None, :],
    ]
    geometry = np.stack([as_tiles(p.astype(np.int32)) for p in planes], axis=1)
    matrices = [jnp.asarray(m, jnp.bfloat16) for m in (to_q, to_k, to_q_rest, to_k_rest)]
    return matrices + [jnp.asarray(geometry)]


def group_constants(levels, columns):
    rows = HALF_LAT * columns * levels
    pick = np.zeros((2 * PAIR, rows), np.float32)
    restore = np.zeros((rows, 2 * WIN_Z * SLOT), np.float32)
    for side in range(2):
        for zw in range(WIN_Z):
            for t in range(GROUP):
                dz, rest = divmod(t, HALF_LAT * HALF_LON)
                di, dj = divmod(rest, HALF_LON)
                z = (WIN_Z * zw + dz + WIN_Z // 2) % levels
                natural = (di * columns + side * HALF_LON + dj) * levels + z
                place = 32 * zw + t if t < 32 else 64 + 4 * zw + t - 32
                pick[side * PAIR + place, natural] = 1.0
                restore[natural, (side * WIN_Z + zw) * SLOT + t] = 1.0
    return jnp.asarray(pick, jnp.bfloat16), jnp.asarray(restore, jnp.bfloat16)


def on_device(
    state_tokens,
    land_mask,
    pad_mask,
    land_embed,
    w_qkv,
    w_proj,
    proj_bias,
    norm_gain,
    norm_shift,
    bias_table,
    index_table,
):
    levels, lat_rows, lon_columns, features = state_tokens.shape
    assert (levels, lat_rows, lon_columns) == (2 * WIN_Z, 2 * WIN_LAT, WIN_LON)
    assert lax.axis_size("lat") == 2 and lax.axis_size("lon") > 2
    highs = -(-bias_table.shape[-1] // LOW)
    pick, restore = group_constants(levels, lon_columns)
    to_q, to_k, to_q_rest, to_k_rest, geometry = bias_constants()
    state = state_tokens.transpose(1, 2, 0, 3)
    table = bias_table.transpose(0, 2, 1, 3)
    inputs = [
        state,
        land_mask,
        land_embed,
        pick,
        w_qkv,
        table,
        index_table,
        to_q,
        to_k,
        to_q_rest,
        to_k_rest,
        geometry,
        pad_mask,
        w_proj,
        proj_bias,
        norm_gain,
        norm_shift,
        restore,
    ]
    bf16, f32, i32 = jnp.bfloat16, jnp.float32, jnp.int32
    dma = pltpu.SemaphoreType.DMA
    scalars = (1, 12)
    copies = [
        (pltpu.SMEM if n in scalars else pltpu.VMEM)(x.shape, x.dtype)
        for n, x in enumerate(inputs)
    ]
    hbm = pl.BlockSpec(memory_space=pl.ANY)
    tokens = levels * lat_rows * lon_columns
    out = pl.pallas_call(
        layer_kernel,
        out_shape=jax.ShapeDtypeStruct(state.shape, bf16),
        in_specs=[hbm] * len(inputs),
        out_specs=hbm,
        scratch_shapes=copies
        + [
            pltpu.VMEM(table.shape[1:], bf16),
            pltpu.VMEM((tokens, features), f32),
            pltpu.VMEM((2, 4 * PAIR, features), bf16),
            pltpu.VMEM((2, 4 * PAIR, features), bf16),
            pltpu.VMEM((4, EDGE_ROWS, features), bf16),
            pltpu.VMEM((2, 4, 3, SLOT, 256), bf16),
            pltpu.VMEM((3, 2, 6, WIN_TOK, 256), bf16),
            pltpu.VMEM((3, 2, 4, 8, 2 * WIDTH), f32),
            pltpu.VMEM((WIN_TOK + 32, 128), i32),
            pltpu.VMEM((WIN_TOK + 32, 128), i32),
            pltpu.VMEM((3, highs * BLOCK // 2, LOW), f32),
            pltpu.VMEM((2, highs * BLOCK, LOW), bf16),
            pltpu.VMEM((2, 2, 3, 2 * GROUP, 8, 256), f32),
            pltpu.VMEM((4, 4 * SLOT, WIDTH), bf16),
            pltpu.VMEM(state.shape, bf16),
            dma((len(inputs),)),
            dma((4,)),
            dma((2, 4)),
            dma((2, 4)),
            dma((2,)),
            dma((4,)),
            dma((4,)),
        ],
        compiler_params=pltpu.CompilerParams(
            collective_id=0, has_side_effects=True, vmem_limit_bytes=56 << 20
        ),
        name="layer",
    )(*inputs)
    return out.transpose(2, 0, 1, 3)


def solution(mesh):
    in_specs = (
        P("member", "lat", "lon", None),
        P("lat", "lon"),
        P(),
        P(),
        P(),
        P(),
        P(),
        P(),
        P(),
        P("lat", None, None, None),
        P(),
    )
    out_specs = P("member", "lat", "lon", None)
    return jax.shard_map(
        on_device, mesh=mesh, in_specs=in_specs, out_specs=out_specs, check_vma=False
    )
```

time: 55.5 us -> 37.8 us (0.68)
  Pallas kernels: 44.4 us -> 35.3 us
  local copies, waits for them, and re-layouts: 10.8 us -> 2.38 us
    pallas_call x1, Pallas kernels: 44.4 us -> 35.3 us  [on_device(): pl.pallas_call(layer_kernel, out_shape=jax.ShapeDtypeStruct(state.shape,...]
    reshape x3 -> x0, local copies, waits for them, and re-layouts: 3.84 us -> none  [on_device(): v.reshape(1, features)]
    pallas_call x1 -> x0, local copies, waits for them, and re-layouts: 2.87 us -> none  [on_device(): pl.pallas_call(layer_kernel, out_shape=jax.ShapeDtypeStruct(state_tokens....]
    unnamed x2 -> x1, local copies, waits for them, and re-layouts: 4.08 us -> 2.38 us
where the time goes in v2:
time: 37.8 us; the launch traced here: 37.7 us
  Pallas kernels  35.3 us (93%)
  local copies, waits for them, and re-layouts  2.38 us (6%)
    pallas_call x1, Pallas kernels, on_device(): pl.pallas_call(layer_kernel, out_shape=jax.ShapeDtypeStruct(state.shape,...  35.3 us
    unnamed x1, local copies, waits for them, and re-layouts  2.38 us

profile of v2, /device:TPU:0, one launch (start us, length us, event | category | flops | bytes accessed | tf_op | source)
XLA Modules:
  0.0 37.7 jit_solution(15987740981700611168)
XLA Ops:
  0.0 35.3 %layer.1 = bf16[12,12,4,768]{3,2,1,0:T(4,128)(2,1)} custom-call(bf16[12,12,4,768]{3,2,1,0:T(4,128)(2,1)} %bitcast.4, s32[12,12]{1,0:T(8,128)} %refs_1_.1, f32[2,768]{1,0:T(2,128)} %refs_2_.1, bf16[144,144]{1,0:T(8,128)(2,1)} %constant.14.clone.refs_3_, bf16[768,1152]{1,0:T(8,128)(2,1)} %refs_4_.1, bf16[2,12,2,3312]{3,2,1,0:T(2,128)(2,1)} %bitcast.5, ...), custom_call_target="tpu_custom_call" | custom-call | tf_op jit(solution)/shard_map/layer/pallas_call | solution.py:622
  35.3 2.4 %copy.20 = bf16[4,12,12,768]{3,0,2,1:T(4,128)(2,1)} copy(bf16[4,12,12,768]{3,0,2,1:T(4,128)(2,1)} %bitcast.3) | data formatting | bytes 1769472

commit v3 on v2

--- a/solution.py
+++ b/solution.py
@@ -24,6 +24,7 @@
 LOW = 256
 SHUT = -1e30
 LOG2E = 1.4426950408889634
+SCALE = HEAD_DIM**-0.5 * LOG2E
 WIDTH = HEADS * HEAD_DIM
 MESH = pl.DeviceIdType.MESH
 
@@ -69,10 +70,12 @@
         ref[WIN_TOK + 16 : WIN_TOK + 32, :] = rest[:, 128:256]
 
 
-def stack_tables(before_ref, own_ref, rows_ref, table_ref):
+def stack_tables(a, before_ref, own_ref, rows_ref, table_ref):
     positions = own_ref.shape[-1]
     heads = own_ref.shape[1]
-    for window in range(3):
+    size = heads * WIN_Z
+    edge = 2 - 2 * a
+    for window in (edge, 1)[: 2 - a]:
         ref = before_ref if window == 0 else own_ref.at[window - 1]
         for k in range(table_ref.shape[1] // BLOCK):
             end = min(positions, (k + 1) * LOW)
@@ -83,15 +86,13 @@
                     part = jnp.concatenate([part, fill], axis=1)
                 row = (k * heads + h) * WIN_Z
                 rows_ref[window, row : row + WIN_Z, :] = part
-    size = heads * WIN_Z
     for k in range(table_ref.shape[1] // BLOCK):
-        own = rows_ref[1, k * size : (k + 1) * size]
-        for a, edge in ((0, 2), (1, 0)):
-            block = jnp.concatenate([rows_ref[edge, k * size : (k + 1) * size], own], axis=0)
-            table_ref[a, k * BLOCK : (k + 1) * BLOCK, :] = block.astype(jnp.bfloat16)
-
-
-def look_up_bias(a, closed, pad_ref, geometry_ref, low_ref, high_ref, table_ref, bias_ref, halfway):
+        both = [rows_ref[window, k * size : (k + 1) * size] for window in (edge, 1)]
+        block = jnp.concatenate(both, axis=0)
+        table_ref[a, k * BLOCK : (k + 1) * BLOCK, :] = block.astype(jnp.bfloat16)
+
+
+def look_up_bias(a, closed, pad_ref, geometry_ref, low_ref, high_ref, table_ref, bias_ref, pause, halfway):
     highs = table_ref.shape[1] // BLOCK
     lat_total = pad_ref.shape[0]
     odd_row = iota((8, LOW), 0) % 2 == 1
@@ -111,13 +112,13 @@
         key_row, same_half, same_level = geometry[0:1], geometry[1:2], geometry[2:3]
         levels = jnp.where(odd_row, jnp.broadcast_to(same_level, (8, LOW)), 1)
         allowed = [levels, levels]
-        if closed:
-            usable = jnp.zeros((1, LOW), jnp.int32)
-            for n in range(WIN_LAT):
-                source = (lat_total - HALF_LAT + n) % lat_total
-                usable = jnp.where(key_row == n, pad_ref[source], usable)
-            usable = jnp.where(usable == 1, same_half, 0)
-            allowed[0] = levels * jnp.broadcast_to(usable, (8, LOW))
+        usable = jnp.zeros((1, LOW), jnp.int32)
+        for n in range(WIN_LAT):
+            source = (lat_total - HALF_LAT + n) % lat_total
+            usable = jnp.where(key_row == n, pad_ref[source], usable)
+        usable = jnp.where(usable == 1, same_half, 0)
+        usable = jnp.maximum(usable, 1 - closed)
+        allowed[0] = levels * jnp.broadcast_to(usable, (8, LOW))
         return [
             jnp.where(allowed[s] == 1, total[s * 3 + kind] * LOG2E, SHUT)
             for s in range(2)
@@ -140,9 +141,9 @@
                 bias_ref[a, s, kind, 2 * p + 1, :, 0:128] = part[:, 128:256]
         return carry
 
-    lax.fori_loop(0, 20, pair, 0, unroll=4)
+    lax.fori_loop(0, pause, pair, 0, unroll=4)
     halfway()
-    lax.fori_loop(20, 36, pair, 0, unroll=4)
+    lax.fori_loop(pause, 36, pair, 0, unroll=4)
     for tile in range(5):
         row = WIN_TOK + a * 5 + tile
 
@@ -178,6 +179,8 @@
         table_ref,
         bias_ref,
         attended_ref,
+        scores_ref,
+        weights_ref,
         result_ref,
         local_sem,
         out_sem,
@@ -340,32 +343,6 @@
         index_planes(
             index_ref, to_q_ref, to_k_ref, to_q_rest_ref, to_k_rest_ref, low_ref, high_ref
         )
-    for side in range(2):
-        empty = pl.multiple_of(64 * lat, 64)
-        for n in range(6):
-            keys_ref[1, side, n, pl.ds(empty, 64), :] = jnp.zeros((64, 256), jnp.bfloat16)
-        for b in range(2):
-            tails_ref[1, side, 2 * lat + b] = jnp.zeros((8, 2 * WIDTH), jnp.float32)
-
-    with jax.named_scope("qkv"):
-        loads[4].wait()
-        for side in range(2):
-            for n in range(2):
-                tokens = tokens_ref[side, 2 * n * PAIR : 2 * (n + 1) * PAIR]
-                qkv = dot(tokens, w_qkv_ref[...])
-                for m in range(2):
-                    slot = 2 * n + m
-                    part = qkv[m * PAIR : (m + 1) * PAIR]
-                    for zw in range(2):
-                        main = part[32 * zw : 32 * zw + 32, 0:WIDTH].astype(jnp.bfloat16)
-                        tail = part[64 + 4 * zw : 68 + 4 * zw, 0:WIDTH].astype(jnp.bfloat16)
-                        for g in range(3):
-                            lanes = slice(128 * g, 128 * g + 128)
-                            out = slice(128 * zw, 128 * zw + 128)
-                            queries_ref[side, slot, g, 0:32, out] = main[:, lanes]
-                            queries_ref[side, slot, g, 32:36, out] = tail[:, lanes]
-                    place(part[:, WIDTH:], min(slot, 2), side, halves[slot], 1 - side)
-
     loads[5].wait()
     with jax.named_scope("barrier"):
         pl.semaphore_wait(barrier, 3)
@@ -376,14 +353,47 @@
     for column in (1, 2):
         lat_copy(column).start()
 
+    for n in range(2):
+        for g in range(3):
+            scores_ref[n, g, :, 128:256] = jnp.full((8 * GROUP, 128), SHUT, jnp.float32)
+    for side in range(2):
+        empty = pl.multiple_of(64 * lat, 64)
+        for n in range(6):
+            keys_ref[1, side, n, pl.ds(empty, 64), :] = jnp.zeros((64, 256), jnp.bfloat16)
+        for b in range(2):
+            tails_ref[1, side, 2 * lat + b] = jnp.zeros((8, 2 * WIDTH), jnp.float32)
+
+    with jax.named_scope("qkv"):
+        loads[4].wait()
+        for side in range(2):
+            for n in range(2):
+                tokens = tokens_ref[side, 2 * n * PAIR : 2 * (n + 1) * PAIR]
+                qkv = dot(tokens, w_qkv_ref[...])
+                for m in range(2):
+                    slot = 2 * n + m
+                    part = qkv[m * PAIR : (m + 1) * PAIR]
+                    queries = part[:, 0:WIDTH].astype(jnp.bfloat16).astype(jnp.float32)
+                    for zw in range(2):
+                        main = queries[32 * zw : 32 * zw + 32]
+                        tail = queries[64 + 4 * zw : 68 + 4 * zw]
+                        for g in range(3):
+                            lanes = slice(128 * g, 128 * g + 128)
+                            out = slice(128 * zw, 128 * zw + 128)
+                            queries_ref[side, slot, g, 0:32, out] = main[:, lanes]
+                            queries_ref[side, slot, g, 32:36, out] = tail[:, lanes]
+                    place(part[:, WIDTH:], min(slot, 2), side, halves[slot], 1 - side)
+
     with jax.named_scope("stack"):
-        table_copy.wait()
-        stack_tables(before_ref, table_own_ref, rows_ref, table_ref)
-
-    def bias(a, closed, halfway):
+        stack_tables(0, before_ref, table_own_ref, rows_ref, table_ref)
+
+    def bias(a, closed, pause, halfway):
         look_up_bias(
-            a, closed, pad_ref, geometry_ref, low_ref, high_ref, table_ref, bias_ref, halfway
+            a, closed, pad_ref, geometry_ref, low_ref, high_ref, table_ref, bias_ref, pause, halfway
         )
+
+    def send_own():
+        for n in (1, 2):
+            lon_copy(far, n).start()
 
     def forward():
         for side in range(2):
@@ -404,40 +414,60 @@
         iota((SLOT, 8 * GROUP), 1) // 8 == iota((SLOT, 8 * GROUP), 0), 1.0, 0.0
     ).astype(jnp.bfloat16)
 
-    def attend(slot, side):
-        window = min(slot, 2) if isinstance(slot, int) else 2
-        a = halves[slot] if isinstance(slot, int) else slot - 2
-        edge_kind = 0 if isinstance(slot, int) and slot < 2 else 1
-        first = (1 - side) * GROUP
+    def place_of(step):
+        kind, side = step // 2, lax.rem(step, 2)
+        slot = jnp.where(kind == 0, 0, jnp.where(kind == 3, 1, kind + 1))
+        return slot, side
+
+    def score(step, g):
+        slot, side = place_of(step)
+        half = jnp.where(slot == 0, lat, jnp.where(slot == 1, other, slot - 2))
+        edge_kind = jnp.where(slot < 2, 0, 1)
+        window = jnp.minimum(slot, 2)
+        first = pl.multiple_of((1 - side) * GROUP, GROUP)
+        spread = jnp.concatenate(
+            [
+                jnp.broadcast_to(queries_ref[side, slot, g, t : t + 1], (8, 256)) * head_mask
+                for t in range(GROUP)
+            ],
+            axis=0,
+        )
+        scores = lax.dot_general(
+            spread.astype(jnp.bfloat16),
+            keys_ref[window, side, g],
+            (((1,), (1,)), ((), ())),
+            preferred_element_type=jnp.float32,
+        )
+        bias = bias_ref[half, edge_kind, g, pl.ds(first, GROUP)].reshape(8 * GROUP, 256)
+        scores_ref[lax.rem(step, 2), g, :, 0:WIN_TOK] = scores * SCALE + bias[:, 0:WIN_TOK]
+
+    def weigh(step, g):
+        scores = scores_ref[lax.rem(step, 2), g]
+        powers = jnp.exp2(scores - jnp.max(scores, axis=-1, keepdims=True))
+        inverse = 1.0 / jnp.sum(powers, axis=-1, keepdims=True)
+        weights_ref[lax.rem(step, 2), g] = (powers * inverse).astype(jnp.bfloat16)
+
+    def mix(step, g):
+        slot, side = place_of(step)
+        window = jnp.minimum(slot, 2)
+        weights = weights_ref[lax.rem(step, 2), g, :, 0:WIN_TOK]
+        mixed = dot(weights, keys_ref[window, side, 3 + g])
+        mixed = (mixed.reshape(GROUP, 8, 256) * head_mask[None]).reshape(8 * GROUP, 256)
+        part = dot(gather_rows, mixed.astype(jnp.bfloat16)).astype(jnp.bfloat16)
+        for zw in range(2):
+            row = pl.multiple_of((side * 2 + zw) * SLOT, SLOT)
+            attended_ref[slot, pl.ds(row, SLOT), 128 * g : 128 * g + 128] = part[
+                :, 128 * zw : 128 * zw + 128
+            ]
+
+    def stages(*parts):
         for g in range(3):
-            key = keys_ref[window, side, g]
-            value = keys_ref[window, side, 3 + g]
-            q = queries_ref[side, slot, g].astype(jnp.float32)[0:GROUP]
-            spread = (q[:, None, :] * head_mask[None]).reshape(8 * GROUP, 256)
-            scores = lax.dot_general(
-                spread.astype(jnp.bfloat16),
-                key,
-                (((1,), (1,)), ((), ())),
-                preferred_element_type=jnp.float32,
-            )
-            bias = bias_ref[a, edge_kind, g, pl.ds(first, GROUP)]
-            bias = bias.reshape(8 * GROUP, 256)[:, 0:WIN_TOK]
-            scores = scores * (HEAD_DIM**-0.5 * LOG2E) + bias
-            powers = jnp.exp2(scores - jnp.max(scores, axis=-1, keepdims=True))
-            inverse = 1.0 / jnp.sum(powers, axis=-1, keepdims=True)
-            weights = (powers * inverse).astype(jnp.bfloat16)
-            mixed = dot(weights, value)
-            mixed = (mixed.reshape(GROUP, 8, 256) * head_mask[None]).reshape(8 * GROUP, 256)
-            part = dot(gather_rows, mixed.astype(jnp.bfloat16)).astype(jnp.bfloat16)
-            for zw in range(2):
-                row = (side * 2 + zw) * SLOT
-                attended_ref[slot, pl.ds(row, SLOT), 128 * g : 128 * g + 128] = part[
-                    :, 128 * zw : 128 * zw + 128
-                ]
-
-    def attend_sides(slot):
-        for side in range(2):
-            attend(slot, side)
+            for stage, step in parts:
+                stage(step, g)
+
+    def advance(step, carry):
+        stages((weigh, step - 1), (score, step), (mix, step - 2))
+        return carry
 
     offset, gain, shift = offset_ref, gain_ref, shift_ref
 
@@ -461,11 +491,12 @@
         out_copy(slot).start()
 
     with jax.named_scope("bias_edge"):
-        bias(lat, False, lambda: None)
-    for n in (1, 2):
-        lon_copy(far, n).start()
+        bias(0, (other == 0).astype(jnp.int32), 32, send_own)
+    with jax.named_scope("stack2"):
+        table_copy.wait()
+        stack_tables(1, before_ref, table_own_ref, rows_ref, table_ref)
     with jax.named_scope("bias_wrap"):
-        bias(other, True, forward)
+        bias(1, (other == 1).astype(jnp.int32), 20, forward)
     for n in range(13, 18):
         loads[n].wait()
     with jax.named_scope("keys_edge"):
@@ -481,7 +512,9 @@
         for side in range(2):
             place_tails(0, side)
     with jax.named_scope("attend_edge"):
-        attend_sides(0)
+        stages((score, 0), (score, 1))
+        stages((weigh, 0), (weigh, 1))
+        stages((mix, 0), (mix, 1))
     lon_copy(far, 3).start()
     with jax.named_scope("finish_edge"):
         finish(0)
@@ -496,11 +529,11 @@
                 place(values[m * PAIR : (m + 1) * PAIR], 2, side, m, side)
             place_tails(2, side)
     with jax.named_scope("attend_own"):
-        def own(slot, carry):
-            attend_sides(slot)
-            return carry
-
-        lax.fori_loop(2, 4, own, 0)
+        stages((score, 2))
+        stages((weigh, 2), (score, 3))
+        lax.fori_loop(4, 6, advance, 0)
+        stages((weigh, 5), (mix, 4))
+        stages((mix, 5))
     with jax.named_scope("finish_own"):
         finish(2)
         finish(3)
@@ -508,12 +541,15 @@
         for side in range(2):
             lon_copy(1 - side, 3).wait_recv()
     with jax.named_scope("keys_wrap"):
-        for side in range(2):
-            values = project(from_lon_ref[side, 64 : 2 * PAIR])
-            place(values[8:80], 1, side, other, side)
+        values = project(from_lon_ref[:, 64 : 2 * PAIR].reshape(2 * EDGE_ROWS, features))
+        for side in range(2):
+            start = EDGE_ROWS * side + 8
+            place(values[start : start + PAIR], 1, side, other, side)
             place_tails(1, side)
     with jax.named_scope("attend_wrap"):
-        attend_sides(1)
+        stages((score, 6), (score, 7))
+        stages((weigh, 6), (weigh, 7))
+        stages((mix, 6), (mix, 7))
     with jax.named_scope("finish_wrap"):
         finish(1)
     with jax.named_scope("drain"):
@@ -617,13 +653,12 @@
         (pltpu.SMEM if n in scalars else pltpu.VMEM)(x.shape, x.dtype)
         for n, x in enumerate(inputs)
     ]
-    hbm = pl.BlockSpec(memory_space=pl.ANY)
     tokens = levels * lat_rows * lon_columns
     out = pl.pallas_call(
         layer_kernel,
-        out_shape=jax.ShapeDtypeStruct(state.shape, bf16),
-        in_specs=[hbm] * len(inputs),
-        out_specs=hbm,
+        out_shape=pltpu.VMEM(state.shape, bf16),
+        in_specs=[pl.BlockSpec(memory_space=pltpu.HBM)] * len(inputs),
+        out_specs=pl.BlockSpec(memory_space=pl.ANY),
         scratch_shapes=copies
         + [
             pltpu.VMEM(table.shape[1:], bf16),
@@ -631,7 +666,7 @@
             pltpu.VMEM((2, 4 * PAIR, features), bf16),
             pltpu.VMEM((2, 4 * PAIR, features), bf16),
             pltpu.VMEM((4, EDGE_ROWS, features), bf16),
-            pltpu.VMEM((2, 4, 3, SLOT, 256), bf16),
+            pltpu.VMEM((2, 4, 3, 40, 256), f32),
             pltpu.VMEM((3, 2, 6, WIN_TOK, 256), bf16),
             pltpu.VMEM((3, 2, 4, 8, 2 * WIDTH), f32),
             pltpu.VMEM((WIN_TOK + 32, 128), i32),
@@ -640,6 +675,8 @@
             pltpu.VMEM((2, highs * BLOCK, LOW), bf16),
             pltpu.VMEM((2, 2, 3, 2 * GROUP, 8, 256), f32),
             pltpu.VMEM((4, 4 * SLOT, WIDTH), bf16),
+            pltpu.VMEM((2, 3, 8 * GROUP, 256), f32),
+            pltpu.VMEM((2, 3, 8 * GROUP, 256), bf16),
             pltpu.VMEM(state.shape, bf16),
             dma((len(inputs),)),
             dma((4,)),

time: 37.8 us -> 33 us (0.87)
  Pallas kernels: 35.3 us -> 31.9 us
  local copies, waits for them, and re-layouts: 2.38 us -> 0.91 us
    pallas_call x1, Pallas kernels: 35.3 us -> 31.9 us  [on_device(): pl.pallas_call(layer_kernel, out_shape=pltpu.VMEM(state.shape, bf16), in_...]
    unnamed x1, local copies, waits for them, and re-layouts: 2.38 us -> 0.91 us
where the time goes in v3:
time: 33 us; the launch traced here: 32.8 us
  Pallas kernels  31.9 us (97%)
  local copies, waits for them, and re-layouts  0.91 us (3%)
    pallas_call x1, Pallas kernels, on_device(): pl.pallas_call(layer_kernel, out_shape=pltpu.VMEM(state.shape, bf16), in_...  31.9 us
    unnamed x1, local copies, waits for them, and re-layouts  0.91 us

profile of v3, /device:TPU:0, one launch (start us, length us, event | category | flops | bytes accessed | tf_op | source)
XLA Modules:
  0.0 32.8 jit_solution(8422064573665588729)
XLA Ops:
  0.0 31.9 %layer.1 = bf16[12,12,4,768]{3,2,1,0:T(4,128)(2,1)S(1)} custom-call(bf16[12,12,4,768]{3,2,1,0:T(4,128)(2,1)} %bitcast.4, s32[12,12]{1,0:T(8,128)} %refs_1_.1, f32[2,768]{1,0:T(2,128)} %refs_2_.1, bf16[144,144]{1,0:T(8,128)(2,1)} %constant.14.clone.refs_3_, bf16[768,1152]{1,0:T(8,128)(2,1)} %refs_4_.1, bf16[2,12,2,3312]{3,2,1,0:T(2,128)(2,1)} %bitcast.5, ...), custom_call_target="tpu_custom_call" | custom-call | tf_op jit(solution)/shard_map/layer/pallas_call | solution.py:657
  31.9 0.9 %copy.20 = bf16[4,12,12,768]{3,0,2,1:T(4,128)(2,1)} copy(bf16[4,12,12,768]{3,0,2,1:T(4,128)(2,1)S(1)} %bitcast.3) | data formatting | bytes 1769472

commit v4 on v3

--- a/solution.py
+++ b/solution.py
@@ -141,9 +141,9 @@
                 bias_ref[a, s, kind, 2 * p + 1, :, 0:128] = part[:, 128:256]
         return carry
 
-    lax.fori_loop(0, pause, pair, 0, unroll=4)
+    lax.fori_loop(0, pause, pair, 0, unroll=6)
     halfway()
-    lax.fori_loop(pause, 36, pair, 0, unroll=4)
+    lax.fori_loop(pause, 36, pair, 0, unroll=6)
     for tile in range(5):
         row = WIN_TOK + a * 5 + tile
 
@@ -162,7 +162,7 @@
 
 def layer_kernel(*refs):
     inputs, refs = refs[:18], refs[18:]
-    out_hbm, refs = refs[0], refs[1:]
+    out_ref, refs = refs[0], refs[1:]
     copies, refs = refs[:18], refs[18:]
     (
         before_ref,
@@ -181,9 +181,7 @@
         attended_ref,
         scores_ref,
         weights_ref,
-        result_ref,
         local_sem,
-        out_sem,
         send_sem,
         recv_sem,
         table_sem,
@@ -337,12 +335,6 @@
                     :, 128 * n : 128 * n + 128
                 ]
 
-    with jax.named_scope("planes"):
-        for n in range(6, 13):
-            loads[n].wait()
-        index_planes(
-            index_ref, to_q_ref, to_k_ref, to_q_rest_ref, to_k_rest_ref, low_ref, high_ref
-        )
     loads[5].wait()
     with jax.named_scope("barrier"):
         pl.semaphore_wait(barrier, 3)
@@ -363,6 +355,12 @@
         for b in range(2):
             tails_ref[1, side, 2 * lat + b] = jnp.zeros((8, 2 * WIDTH), jnp.float32)
 
+    with jax.named_scope("planes"):
+        for n in range(6, 13):
+            loads[n].wait()
+        index_planes(
+            index_ref, to_q_ref, to_k_ref, to_q_rest_ref, to_k_rest_ref, low_ref, high_ref
+        )
     with jax.named_scope("qkv"):
         loads[4].wait()
         for side in range(2):
@@ -465,15 +463,7 @@
             for stage, step in parts:
                 stage(step, g)
 
-    def advance(step, carry):
-        stages((weigh, step - 1), (score, step), (mix, step - 2))
-        return carry
-
     offset, gain, shift = offset_ref, gain_ref, shift_ref
-
-    def out_copy(slot):
-        rows = pl.ds(quarters[slot] * HALF_LAT, HALF_LAT)
-        return pltpu.make_async_copy(result_ref.at[rows], out_hbm.at[rows], out_sem.at[slot])
 
     def finish(slot):
         quarter = quarters[slot]
@@ -487,16 +477,15 @@
         for n in range(HALF_LAT * lon_columns):
             i, j = divmod(n, lon_columns)
             part = result[n * levels : (n + 1) * levels]
-            result_ref[quarter * HALF_LAT + i, j] = part.astype(jnp.bfloat16)
-        out_copy(slot).start()
+            out_ref[quarter * HALF_LAT + i, j] = part.astype(jnp.bfloat16)
 
     with jax.named_scope("bias_edge"):
-        bias(0, (other == 0).astype(jnp.int32), 32, send_own)
+        bias(0, (other == 0).astype(jnp.int32), 36, send_own)
     with jax.named_scope("stack2"):
         table_copy.wait()
         stack_tables(1, before_ref, table_own_ref, rows_ref, table_ref)
     with jax.named_scope("bias_wrap"):
-        bias(1, (other == 1).astype(jnp.int32), 20, forward)
+        bias(1, (other == 1).astype(jnp.int32), 18, forward)
     for n in range(13, 18):
         loads[n].wait()
     with jax.named_scope("keys_edge"):
@@ -529,11 +518,11 @@
                 place(values[m * PAIR : (m + 1) * PAIR], 2, side, m, side)
             place_tails(2, side)
     with jax.named_scope("attend_own"):
-        stages((score, 2))
-        stages((weigh, 2), (score, 3))
-        lax.fori_loop(4, 6, advance, 0)
-        stages((weigh, 5), (mix, 4))
-        stages((mix, 5))
+        stages((score, 2), (score, 3))
+        stages((weigh, 2), (weigh, 3))
+        stages((mix, 2), (score, 4), (mix, 3), (score, 5))
+        stages((weigh, 4), (weigh, 5))
+        stages((mix, 4), (mix, 5))
     with jax.named_scope("finish_own"):
         finish(2)
         finish(3)
@@ -553,8 +542,6 @@
     with jax.named_scope("finish_wrap"):
         finish(1)
     with jax.named_scope("drain"):
-        for slot in range(4):
-            out_copy(slot).wait()
         for side in range(2):
             for n in range(4):
                 lon_copy(side, n).wait_send()
@@ -658,7 +645,7 @@
         layer_kernel,
         out_shape=pltpu.VMEM(state.shape, bf16),
         in_specs=[pl.BlockSpec(memory_space=pltpu.HBM)] * len(inputs),
-        out_specs=pl.BlockSpec(memory_space=pl.ANY),
+        out_specs=pl.BlockSpec(memory_space=pltpu.VMEM),
         scratch_shapes=copies
         + [
             pltpu.VMEM(table.shape[1:], bf16),
@@ -677,9 +664,7 @@
             pltpu.VMEM((4, 4 * SLOT, WIDTH), bf16),
             pltpu.VMEM((2, 3, 8 * GROUP, 256), f32),
             pltpu.VMEM((2, 3, 8 * GROUP, 256), bf16),
-            pltpu.VMEM(state.shape, bf16),
             dma((len(inputs),)),
-            dma((4,)),
             dma((2, 4)),
             dma((2, 4)),
             dma((2,)),

time: 33 us -> 30.4 us (0.921)
  Pallas kernels: 31.9 us -> 29.4 us
    pallas_call x1, Pallas kernels: 31.9 us -> 29.4 us  [on_device(): pl.pallas_call(layer_kernel, out_shape=pltpu.VMEM(state.shape, bf16), in_...]
where the time goes in v4:
time: 30.4 us; the launch traced here: 30.3 us
  Pallas kernels  29.4 us (97%)
  local copies, waits for them, and re-layouts  0.91 us (3%)
    pallas_call x1, Pallas kernels, on_device(): pl.pallas_call(layer_kernel, out_shape=pltpu.VMEM(state.shape, bf16), in_...  29.4 us
    unnamed x1, local copies, waits for them, and re-layouts  0.91 us

profile of v4, /device:TPU:0, one launch (start us, length us, event | category | flops | bytes accessed | tf_op | source)
XLA Modules:
  0.0 30.3 jit_solution(12870694709497091049)
XLA Ops:
  0.0 29.4 %layer.1 = bf16[12,12,4,768]{3,2,1,0:T(4,128)(2,1)S(1)} custom-call(bf16[12,12,4,768]{3,2,1,0:T(4,128)(2,1)} %bitcast.4, s32[12,12]{1,0:T(8,128)} %refs_1_.1, f32[2,768]{1,0:T(2,128)} %refs_2_.1, bf16[144,144]{1,0:T(8,128)(2,1)} %constant.14.clone.refs_3_, bf16[768,1152]{1,0:T(8,128)(2,1)} %refs_4_.1, bf16[2,12,2,3312]{3,2,1,0:T(2,128)(2,1)} %bitcast.5, ...), custom_call_target="tpu_custom_call" | custom-call | tf_op jit(solution)/shard_map/layer/pallas_call | solution.py:644
  29.4 0.9 %copy.20 = bf16[4,12,12,768]{3,0,2,1:T(4,128)(2,1)} copy(bf16[4,12,12,768]{3,0,2,1:T(4,128)(2,1)S(1)} %bitcast.3) | data formatting | bytes 1769472
